TPU v7x, 768 devices: a whole 4x8x12 slice. The times are simulated.
768 devices in a mesh: dp: 4 (over y_lo, core), expert: 48 (over z, y_hi), tensor: 4 (over x).
Axes of the slice: x: 4, y: 8 (y_hi: 4, y_lo: 2; y = y_hi * 2 + y_lo), z: 12, core: 2. Of those that a mesh axis runs over, the one named last changes fastest.
Arguments:
- tokens: bfloat16 [3072, 3072], P(('dp', 'expert')), may hold values from -45 to 45
- cotangent: bfloat16 [3072, 3072], P(('dp', 'expert')), may hold values from -6 to 6
- gain: float32 [3072], replicated, may hold values from 0.5 to 1.5
- w_router: bfloat16 [3072, 8], replicated, may hold values from -0.109375 to 0.109375
- w_gate: bfloat16 [48, 3072, 1536], P('expert', None, 'tensor'), may hold values from -0.109375 to 0.109375
- w_up: bfloat16 [48, 3072, 1536], P('expert', None, 'tensor'), may hold values from -0.109375 to 0.109375
- w_down: bfloat16 [48, 1536, 3072], P('expert', 'tensor'), may hold values from -0.0625 to 0.0625
- expert_ids: int32 [3072, 2], P(('dp', 'expert')), may hold values from 0 to 7, as said below
- slots: int32 [3072, 2], P(('dp', 'expert')), may hold values from 0 to 3, as said below
Outputs:
- mixed: bfloat16 [3072, 3072], P(('dp', 'expert'))
- grad_tokens: bfloat16 [3072, 3072], P(('dp', 'expert'))
- grad_router: float32 [3072, 8], replicated
- grad_gain: float32 [3072], replicated
Inputs may be any that keep to these rules, and one draw needn't show every extreme that they name: `expert_ids`: within each aligned block of 16 rows (one group), every expert is named exactly 4 times, and a row's two ids differ. Within each aligned block of 16 rows, the choices naming one expert hold its slots 0 to 3, each once.
All inputs are finite; a program needn't handle non-finite values.
Results may differ from a plain program's by a relative error of at most 0.0095.
Values may be sent and summed in bfloat16 or wider, within the bound.
A program may use at most 64 MiB of HBM per device.

v0:
```python
import jax
import jax.numpy as jnp
from jax import lax
from jax.sharding import PartitionSpec as P

epsilon = 1e-05


def in_blocks(value, dim, devices):
    before, after = (value.shape[:dim], value.shape[dim + 1 :])
    return jnp.moveaxis(value.reshape(*before, devices, -1, *after), dim, 0)


def summed_on_arrival(value, axis, dim):
    parts = in_blocks(value, dim, lax.axis_size(axis))
    arrived = lax.all_to_all(parts, axis, split_axis=0, concat_axis=0, tiled=True)
    return arrived.astype(jnp.float32).sum(axis=0)


def in_one(arrays, axis):
    line, at, finished = (jnp.concatenate([a.reshape(-1) for a in arrays]), 0, [])
    so_far = lax.psum(line, axis)
    for a in arrays:
        finished.append(so_far[at : at + a.size].reshape(a.shape))
        at += a.size
    return tuple(finished)


def pack_rows(select, values):
    return jnp.einsum("tcr,tcd->rd", select, values, preferred_element_type=jnp.float32).astype(
        jnp.bfloat16
    )


def repeat_blocks(packed, experts, copies):
    feature_width = packed.shape[1]
    blocks = packed.reshape(experts, 1, -1, feature_width)
    blocks = jnp.broadcast_to(blocks, (experts, copies, blocks.shape[2], feature_width))
    return blocks.reshape(experts * copies, -1, feature_width)


def to_experts(packed, experts, copies):
    slice_width = packed.shape[1] // lax.axis_size("tensor")
    feature_slice = lax.dynamic_slice_in_dim(
        packed, lax.axis_index("tensor") * slice_width, slice_width, 1
    )
    arrived = lax.all_to_all(
        repeat_blocks(feature_slice, experts, copies),
        "expert",
        split_axis=0,
        concat_axis=0,
        tiled=True,
    )
    arrived = lax.all_gather(arrived, "tensor", axis=2, tiled=True)
    return arrived.reshape(-1, packed.shape[1])


def from_experts(partial_value, row_index, experts, copies):
    partial_value = summed_on_arrival(partial_value.astype(jnp.bfloat16), "tensor", 1)
    feature_width = partial_value.shape[1]
    returned_rows = lax.all_to_all(
        partial_value.reshape(experts * copies, -1, feature_width),
        "expert",
        split_axis=0,
        concat_axis=0,
        tiled=True,
    )
    summed = jnp.sum(returned_rows.reshape(experts, copies, -1, feature_width), axis=1).reshape(
        -1, feature_width
    )
    picked = summed[row_index]
    picked = lax.all_gather(picked.astype(jnp.bfloat16), "tensor", axis=2, tiled=True).astype(
        picked.dtype
    )
    return picked


def shards(tokens, cotangent, gain, w_router, w_gate, w_up, w_down, expert_ids, slots):
    experts = w_router.shape[1]
    copies = lax.axis_size("expert") // experts
    token_count = tokens.shape[0]
    capacity = 2 * token_count // experts
    floats = tokens.astype(jnp.float32)
    inv_rms = lax.rsqrt(jnp.mean(floats * floats, axis=1, keepdims=True) + epsilon)
    normed = (floats * inv_rms * gain).astype(jnp.bfloat16)
    logits = jnp.dot(normed, w_router, preferred_element_type=jnp.float32)
    chosen_logits = jnp.take_along_axis(logits, expert_ids, axis=1)
    first_prob = jax.nn.sigmoid(chosen_logits[:, 0] - chosen_logits[:, 1])
    pair_probs = jnp.stack([first_prob, 1.0 - first_prob], axis=1)
    row_index = expert_ids * capacity + slots
    select = (
        row_index[:, :, None] == jnp.arange(experts * capacity, dtype=jnp.int32)[None, None, :]
    ).astype(jnp.bfloat16)
    feature_width = tokens.shape[1]
    inputs = to_experts(
        pack_rows(select, jnp.broadcast_to(normed[:, None, :], (token_count, 2, feature_width))),
        experts,
        copies,
    )
    gate_matrix = w_gate[0]
    up_matrix = w_up[0]
    down_matrix = w_down[0]
    gate_pre = jnp.dot(inputs, gate_matrix, preferred_element_type=jnp.float32)
    up_pre = jnp.dot(inputs, up_matrix, preferred_element_type=jnp.float32)
    activated = (jax.nn.silu(gate_pre) * up_pre).astype(jnp.bfloat16)
    chosen = from_experts(
        jnp.dot(activated, down_matrix, preferred_element_type=jnp.float32),
        row_index,
        experts,
        copies,
    )
    mixed = (floats + jnp.sum(pair_probs[:, :, None] * chosen, axis=1)).astype(jnp.bfloat16)
    upstream = cotangent.astype(jnp.float32)
    sent_grads = (pair_probs[:, :, None] * upstream[:, None, :]).astype(jnp.bfloat16)
    grad_outputs = to_experts(pack_rows(select, sent_grads), experts, copies)
    grad_act = jnp.dot(grad_outputs, down_matrix.T, preferred_element_type=jnp.float32)
    sigmoid_gate = jax.nn.sigmoid(gate_pre)
    grad_gate = (grad_act * up_pre * sigmoid_gate * (1.0 + gate_pre * (1.0 - sigmoid_gate))).astype(
        jnp.bfloat16
    )
    grad_up = (grad_act * jax.nn.silu(gate_pre)).astype(jnp.bfloat16)
    grad_inputs = jnp.dot(grad_gate, gate_matrix.T, preferred_element_type=jnp.float32) + jnp.dot(
        grad_up, up_matrix.T, preferred_element_type=jnp.float32
    )
    grad_mixture = jnp.sum(from_experts(grad_inputs, row_index, experts, copies), axis=1)
    grad_probs = jnp.sum(upstream[:, None, :] * chosen, axis=2)
    grad_first = first_prob * (1.0 - first_prob) * (grad_probs[:, 0] - grad_probs[:, 1])
    columns = jnp.arange(experts, dtype=jnp.int32)[None, :]
    grad_logits = grad_first[:, None] * (
        (expert_ids[:, 0:1] == columns).astype(jnp.float32)
        - (expert_ids[:, 1:2] == columns).astype(jnp.float32)
    )
    grad_normed = grad_mixture + jnp.dot(
        grad_logits, w_router.astype(jnp.float32).T, precision=lax.Precision.HIGHEST
    )
    router_part = jnp.dot(
        normed.astype(jnp.float32).T, grad_logits, precision=lax.Precision.HIGHEST
    )
    gain_part = jnp.sum(grad_normed * floats * inv_rms, axis=0)
    grad_router, grad_gain = in_one((router_part, gain_part), ("dp", "expert"))
    grad_scaled = grad_normed * gain
    cubed = inv_rms * inv_rms * inv_rms
    grad_tokens = (
        upstream
        + inv_rms * grad_scaled
        - floats * cubed * jnp.mean(grad_scaled * floats, axis=1, keepdims=True)
    ).astype(jnp.bfloat16)
    return (mixed, grad_tokens, grad_router, grad_gain)


def solution(mesh):
    return jax.shard_map(
        shards,
        mesh=mesh,
        in_specs=(
            P(("dp", "expert"), None),
            P(("dp", "expert"), None),
            P(),
            P(),
            P("expert", None, "tensor"),
            P("expert", None, "tensor"),
            P("expert", "tensor", None),
            P(("dp", "expert"), None),
            P(("dp", "expert"), None),
        ),
        out_specs=(P(("dp", "expert"), None), P(("dp", "expert"), None), P(), P()),
        check_vma=False,
    )
```

profile of v0, /device:TPU:1, one launch (start us, length us, event | category | flops | bytes accessed | tf_op | source)
XLA Modules:
  0.0 525.3 jit_solution(11108420252128853110)
XLA Ops:
  7.2 1.2 fusion.14
  8.4 0.5 multiply_multiply_fusion
  8.9 0.7 bitcast_or_fusion
  9.6 0.7 compare_select_fusion
  10.3 0.1 copy.59
  10.4 0.1 reshape.122
  10.5 1.0 fusion.16
  11.5 1.0 fusion.42
  12.5 0.7 gather_fusion.2
  13.2 0.1 reshape.125
  13.3 0.1 copy.60
  13.4 0.3 convolution_bitcast_fusion.1
  13.8 0.3 convolution_bitcast_fusion
  14.2 0.1 broadcast_in_dim.19
  14.2 41.5 %all_to_all.30 = bf16[48,4,768]{2,1,0:T(4,128)(2,1)} all-to-all(bf16[48,4,768]{2,1,0:T(4,128)(2,1)S(1)} %bitcast.60), channel_id=1, replica_groups=mesh['dp'=4,'expert'=48,'tensor'=4] {'expert'}, dimensions={0} | all-to-all | bytes 589824 | tf_op jit(solution)/shard_map/all_to_all | solution.py:47
  55.8 0.0 all-gather.5.cloned.1.call-start
  55.9 0.1 broadcast_in_dim.22
  56.0 23.4 %all_to_all.31 = bf16[48,4,768]{2,1,0:T(4,128)(2,1)} all-to-all(bf16[48,4,768]{2,1,0:T(4,128)(2,1)S(1)} %bitcast.61), channel_id=1, replica_groups=mesh['dp'=4,'expert'=48,'tensor'=4] {'expert'}, dimensions={0} | all-to-all | bytes 589824 | tf_op jit(solution)/shard_map/all_to_all | solution.py:47
  79.4 3.1 reshape.94
  82.5 2.9 fusion.9
  85.5 0.1 copy-done.12
  85.6 0.8 fusion.5
  86.4 0.8 convolution_convert_fusion
  87.2 1.1 copy.79
  88.3 4.0 all-to-all-start.1
  92.3 26.7 %all-gather.5.cloned.1.call-done = bf16[48,4,3072]{2,1,0:T(4,128)(2,1)} async-done(((bf16[48,4,768]{2,1,0:T(4,128)(2,1)}), bf16[48,4,3072]{2,1,0:T(4,128)(2,1)}) %all-gather.5.cloned.1.call-update) | async-done | bytes 1179664 | tf_op jit(solution)/shard_map/all_gather | solution.py:54
  119.0 3.1 reshape.100
  122.2 2.4 fusion.1
  124.6 1.0 fusion.7
  125.6 0.7 copy-done.4
  126.2 1.0 fusion
  127.2 1.1 copy.78
  128.3 4.3 all-to-all-start.4
  132.6 1.0 convert_reduce_fusion.1
  133.6 2.1 reshape.96
  135.6 13.1 %all-to-all-done.4 = bf16[4,192,768]{2,1,0:T(8,128)(2,1)} async-done(((bf16[4,192,768]{2,1,0:T(8,128)(2,1)}), bf16[4,192,768]{2,1,0:T(8,128)(2,1)}, u32[]{:S(2)}, u32[]{:S(2)}) %all-to-all-start.4) | async-done | bytes 1179680 | tf_op jit(solution)/shard_map/all_to_all | solution.py:16
  148.7 13.1 %all-to-all-start.2 = ((f32[48,4,768]{2,1,0:T(4,128)}), f32[48,4,768]{2,1,0:T(4,128)S(1)}, u32[]{:S(2)}, u32[]{:S(2)}) async-start(f32[48,4,768]{2,1,0:T(4,128)} %reshape.96), calls=%async_computation.2 | async-start | bytes 1179648 | tf_op jit(solution)/shard_map/all_to_all | solution.py:61
  161.8 1.5 convert_reduce_fusion
  163.3 1.0 reshape.102
  164.3 25.7 %all-to-all-done.2 = f32[48,4,768]{2,1,0:T(4,128)S(1)} async-done(((f32[48,4,768]{2,1,0:T(4,128)}), f32[48,4,768]{2,1,0:T(4,128)S(1)}, u32[]{:S(2)}, u32[]{:S(2)}) %all-to-all-start.2) | async-done | bytes 589856 | tf_op jit(solution)/shard_map/all_to_all | solution.py:61
  190.0 0.8 copy-done.5
  190.8 5.6 %all-to-all-start.5 = ((f32[48,4,768]{2,1,0:T(4,128)}), f32[48,4,768]{2,1,0:T(4,128)S(1)}, u32[]{:S(2)}, u32[]{:S(2)}) async-start(f32[48,4,768]{2,1,0:T(4,128)} %reshape.102), calls=%async_computation.5 | async-start | bytes 1179648 | tf_op jit(solution)/shard_map/all_to_all | solution.py:61
  196.5 0.1 copy.64
  196.6 0.1 reshape.108
  196.7 1.2 reduce_sum.92
  197.9 0.6 gather_fusion
  198.6 10.3 %all_gather.13 = bf16[16,2,3072]{2,0,1:T(8,128)(2,1)S(1)} all-gather(bf16[16,2,768]{2,0,1:T(8,128)(2,1)S(1)} %copy.65), channel_id=1, replica_groups=mesh['dp'=4,'expert'=48,'tensor'=4] {'tensor'}, dimensions={2}, use_global_device_ids=true | all-gather | bytes 245760 | tf_op jit(solution)/shard_map/all_gather | solution.py:72
  208.9 1.1 fusion.12
  210.0 0.6 copy-done.19
  210.6 3.0 fusion.30
  213.6 2.1 reshape.105
  215.8 8.7 %all-to-all-done.5 = f32[48,4,768]{2,1,0:T(4,128)S(1)} async-done(((f32[48,4,768]{2,1,0:T(4,128)}), f32[48,4,768]{2,1,0:T(4,128)S(1)}, u32[]{:S(2)}, u32[]{:S(2)}) %all-to-all-start.5) | async-done | bytes 589856 | tf_op jit(solution)/shard_map/all_to_all | solution.py:61
  224.5 0.1 reduce_sum.95
  224.6 0.6 gather_fusion.1
  225.2 9.4 %all_gather.15 = bf16[16,2,3072]{2,1,0:T(2,128)(2,1)S(1)} all-gather(bf16[16,2,768]{2,1,0:T(2,128)(2,1)S(1)} %reshape.133), channel_id=1, replica_groups=mesh['dp'=4,'expert'=48,'tensor'=4] {'tensor'}, dimensions={2}, use_global_device_ids=true | all-gather | bytes 245760 | tf_op jit(solution)/shard_map/all_gather | solution.py:72
  234.6 0.5 convert_reduce_fusion.2
  235.1 1.3 fusion.23
  236.4 0.6 pad_maximum_fusion
  237.1 1.4 fusion.20
  238.6 273.5 %all-reduce.2.cloned.1.call-done = f32[27648]{0:T(1024)} async-done(((f32[27648]{0:T(1024)}), f32[27648]{0:T(1024)}) %all-reduce.2.cloned.1.call-update) | async-done | bytes 110608 | tf_op jit(solution)/shard_map/psum | solution.py:22
  512.1 0.9 slice.49
  513.0 2.0 slice.41
  515.0 2.5 copy.70
  517.5 1.3 slice.50
  (61 shorter events, 0.5 us)
Async XLA Ops:
  7.2 79.2 %copy-start = (bf16[1,384,3072]{2,1,0:T(8,128)(2,1)S(1)}, bf16[1,384,3072]{2,1,0:T(8,128)(2,1)}, u32[]{:S(2)}) copy-start(bf16[1,384,3072]{2,1,0:T(8,128)(2,1)} %param.15) | copy-start | bytes 7077892
  7.2 72.2 %all-gather.3.cloned.1.call-start = ((), (), s32[]{:S(2)}) async-start(), calls=%async_computation.6 | async-start | bytes 1474560 | tf_op jit(solution)/shard_map/all_gather | solution.py:54
  8.9 1.6 copy-start.20
  11.5 1.9 copy-start.9
  12.5 0.9 copy-start.16
  12.5 0.9 copy-start.13
  13.4 69.1 %copy-start.7 = (f32[16,3072]{1,0:T(8,128)}, f32[16,3072]{1,0:T(8,128)S(1)}, u32[]{:S(2)}) copy-start(f32[16,3072]{1,0:T(8,128)S(1)} %convert_element_type.75) | copy-start | bytes 589828
  55.8 63.2 %all-gather.5.cloned.1.call-start = ((), (), s32[]{:S(2)}) async-start(), calls=%async_computation.7 | async-start | bytes 1474560 | tf_op jit(solution)/shard_map/all_gather | solution.py:54
  82.5 3.0 copy-start.3
  82.5 3.0 copy-start.12
  85.6 1.6 copy-start.1
  86.4 1.9 copy-start.10
  88.3 40.0 %all-to-all-start.1 = ((bf16[4,192,768]{2,1,0:T(8,128)(2,1)}), bf16[4,192,768]{2,1,0:T(8,128)(2,1)S(1)}, u32[]{:S(2)}, u32[]{:S(2)}) async-start(bf16[4,192,768]{2,1,0:T(8,128)(2,1)} %bitcast.55), calls=%async_computation.1 | async-start | bytes 2359296 | tf_op jit(solution)/shard_map/all_to_all | solution.py:16
  122.2 2.4 copy-start.2
  122.2 2.4 copy-start.6
  122.2 2.4 copy-start.11
  124.6 1.7 copy-start.4
  128.3 20.4 %all-to-all-start.4 = ((bf16[4,192,768]{2,1,0:T(8,128)(2,1)}), bf16[4,192,768]{2,1,0:T(8,128)(2,1)}, u32[]{:S(2)}, u32[]{:S(2)}) async-start(bf16[4,192,768]{2,1,0:T(8,128)(2,1)} %bitcast.56), calls=%async_computation.4 | async-start | bytes 2359296 | tf_op jit(solution)/shard_map/all_to_all | solution.py:16
  148.7 41.3 %all-to-all-start.2 = ((f32[48,4,768]{2,1,0:T(4,128)}), f32[48,4,768]{2,1,0:T(4,128)S(1)}, u32[]{:S(2)}, u32[]{:S(2)}) async-start(f32[48,4,768]{2,1,0:T(4,128)} %reshape.96), calls=%async_computation.2 | async-start | bytes 1179648 | tf_op jit(solution)/shard_map/all_to_all | solution.py:61
  190.0 0.8 copy-start.5
  190.8 33.6 %all-to-all-start.5 = ((f32[48,4,768]{2,1,0:T(4,128)}), f32[48,4,768]{2,1,0:T(4,128)S(1)}, u32[]{:S(2)}, u32[]{:S(2)}) async-start(f32[48,4,768]{2,1,0:T(4,128)} %reshape.102), calls=%async_computation.5 | async-start | bytes 1179648 | tf_op jit(solution)/shard_map/all_to_all | solution.py:61
  196.4 315.6 %all-reduce.2.cloned.1.call-start = ((), (), s32[]{:S(2)}) async-start(), calls=%async_computation.8 | async-start | bytes 221184 | tf_op jit(solution)/shard_map/psum | solution.py:22
  196.7 13.3 %copy-start.17 = (s32[16]{0:T(128)}, s32[16]{0:T(128)S(1)}, u32[]{:S(2)}) copy-start(s32[16]{0:T(128)S(1)} %get-tuple-element.30) | copy-start | bytes 196
  196.7 13.3 %copy-start.18 = (s32[16]{0:T(128)}, s32[16]{0:T(128)S(1)}, u32[]{:S(2)}) copy-start(s32[16]{0:T(128)S(1)} %get-tuple-element.31) | copy-start | bytes 196
  210.0 0.6 copy-start.19
  210.6 24.5 %copy-start.8 = (bf16[16,3072]{1,0:T(8,128)(2,1)S(1)}, bf16[16,3072]{1,0:T(8,128)(2,1)}, u32[]{:S(2)}) copy-start(bf16[16,3072]{1,0:T(8,128)(2,1)} %param.9) | copy-start | bytes 294916
  210.6 24.5 %copy-start.15 = (f32[3072]{0:T(1024)S(1)}, f32[3072]{0:T(1024)}, u32[]{:S(2)}) copy-start(f32[3072]{0:T(1024)} %param.11) | copy-start | bytes 36868
  213.6 23.5 %copy-start.14 = (bf16[16,3072]{1,0:T(8,128)(2,1)S(1)}, bf16[16,3072]{1,0:T(8,128)(2,1)}, u32[]{:S(2)}) copy-start(bf16[16,3072]{1,0:T(8,128)(2,1)} %param.10) | copy-start | bytes 294916
Sparse Core Ops, SparseCore 0:
  55.9 22.7 all-gather.2
  81.1 37.8 all-gather.4
  237.2 274.7 all-reduce.1
where the time goes:
time: 527 us; the launch traced here: 525 us
  waiting for transfers between devices  348 us (66%)
  blocking collectives  84.6 us (16%)
  starting transfers between devices  27.1 us (5%)
  local copies, waits for them, and re-layouts  25.3 us (5%)
  matrix products  14.8 us (3%)
  between operations  14.2 us (3%)
  other arithmetic  11.6 us (2%)
    psum x1, waiting for transfers between devices, in_one(): so_far = lax.psum(line, axis)  273 us
    all_to_all x2, blocking collectives, to_experts(): lax.all_to_all(repeat_blocks(feature_slice, experts, copies), 'expert', s...  64.9 us
    all_to_all x2, waiting for transfers between devices, from_experts(): lax.all_to_all(partial_value.reshape(experts * copies, -1, feature_width)...  34.4 us
    all_gather x2, waiting for transfers between devices, to_experts(): arrived = lax.all_gather(arrived, 'tensor', axis=2, tiled=True)  26.8 us
    all_gather x2, blocking collectives, from_experts(): lax.all_gather(picked.astype(jnp.bfloat16), 'tensor', axis=2, tiled=True)  19.7 us
    all_to_all x2, starting transfers between devices, from_experts(): lax.all_to_all(partial_value.reshape(experts * copies, -1, feature_width)...  18.7 us
    all_to_all x2, waiting for transfers between devices, summed_on_arrival(): lax.all_to_all(parts, axis, split_axis=0, concat_axis=0, tiled=True)  13.1 us
  transfers between devices with their start and end apart: 7, of which 5 were waited for; matrix products, arithmetic and copies ran while one was open for 6% of the time, Pallas kernels for 0%

commit v1 on v0

--- a/solution.py
+++ b/solution.py
@@ -19,6 +19,9 @@
 
 def in_one(arrays, axis):
     line, at, finished = (jnp.concatenate([a.reshape(-1) for a in arrays]), 0, [])
+    quarter = line.size // lax.axis_size("tensor")
+    owner = jnp.arange(line.size, dtype=jnp.int32) // quarter
+    line = jnp.where(owner == lax.axis_index("tensor"), line, 0.0)
     so_far = lax.psum(line, axis)
     for a in arrays:
         finished.append(so_far[at : at + a.size].reshape(a.shape))
@@ -59,12 +62,12 @@
     partial_value = summed_on_arrival(partial_value.astype(jnp.bfloat16), "tensor", 1)
     feature_width = partial_value.shape[1]
     returned_rows = lax.all_to_all(
-        partial_value.reshape(experts * copies, -1, feature_width),
+        partial_value.astype(jnp.bfloat16).reshape(experts * copies, -1, feature_width),
         "expert",
         split_axis=0,
         concat_axis=0,
         tiled=True,
-    )
+    ).astype(jnp.float32)
     summed = jnp.sum(returned_rows.reshape(experts, copies, -1, feature_width), axis=1).reshape(
         -1, feature_width
     )
@@ -137,7 +140,7 @@
         normed.astype(jnp.float32).T, grad_logits, precision=lax.Precision.HIGHEST
     )
     gain_part = jnp.sum(grad_normed * floats * inv_rms, axis=0)
-    grad_router, grad_gain = in_one((router_part, gain_part), ("dp", "expert"))
+    grad_router, grad_gain = in_one((router_part, gain_part), ("dp", "expert", "tensor"))
     grad_scaled = grad_normed * gain
     cubed = inv_rms * inv_rms * inv_rms
     grad_tokens = (

time: 527 us -> 694 us (1.32)
  waiting for transfers between devices: 348 us -> 519 us
    psum x1, waiting for transfers between devices: 273 us -> 461 us  [in_one(): so_far = lax.psum(line, axis)]
    all_to_all x2, waiting for transfers between devices: 34.4 us -> 17.7 us  [from_experts(): lax.all_to_all(partial_value.astype(jnp.bfloat16).reshape(experts * copie...]
  transfers between devices with their start and end apart: 7 -> 7, of which waited for: 5 -> 5; matrix products, arithmetic and copies ran while one was open for 6% -> 4% of each run, Pallas kernels for 0% -> 0%
where the time goes in v1:
time: 694 us; the launch traced here: 692 us
  waiting for transfers between devices  519 us (75%)
  blocking collectives  84.5 us (12%)
  starting transfers between devices  27.6 us (4%)
  local copies, waits for them, and re-layouts  24.2 us (3%)
  between operations  14.2 us (2%)
  matrix products  13 us (2%)
  other arithmetic  9.55 us (1%)
    psum x1, waiting for transfers between devices, in_one(): so_far = lax.psum(line, axis)  461 us
    all_to_all x2, blocking collectives, to_experts(): lax.all_to_all(repeat_blocks(feature_slice, experts, copies), 'expert', s...  64.9 us
    all_gather x2, waiting for transfers between devices, to_experts(): arrived = lax.all_gather(arrived, 'tensor', axis=2, tiled=True)  26.8 us
    all_gather x2, blocking collectives, from_experts(): lax.all_gather(picked.astype(jnp.bfloat16), 'tensor', axis=2, tiled=True)  19.6 us
    all_to_all x2, starting transfers between devices, from_experts(): lax.all_to_all(partial_value.astype(jnp.bfloat16).reshape(experts * copie...  19.2 us
    all_to_all x2, waiting for transfers between devices, from_experts(): lax.all_to_all(partial_value.astype(jnp.bfloat16).reshape(experts * copie...  17.7 us
  transfers between devices with their start and end apart: 7, of which 5 were waited for; matrix products, arithmetic and copies ran while one was open for 4% of the time, Pallas kernels for 0%

profile of v1, /device:TPU:1, one launch (start us, length us, event | category | flops | bytes accessed | tf_op | source)
XLA Modules:
  0.0 692.2 jit_solution(4296905241862353886)
XLA Ops:
  7.2 0.0 all-gather.3.cloned.1.call-start
  7.2 1.2 fusion.14
  8.4 0.5 multiply_multiply_fusion
  8.9 0.7 bitcast_or_fusion
  9.6 1.3 compare_select_fusion
  10.9 0.1 copy.59
  11.0 0.1 reshape.134
  11.1 1.0 fusion.16
  12.1 1.0 fusion.46
  13.0 0.7 gather_fusion.2
  13.7 0.1 reshape.137
  13.8 0.1 copy.60
  14.0 0.3 convolution_bitcast_fusion.1
  14.3 0.3 convolution_bitcast_fusion
  14.7 0.1 broadcast_in_dim.22
  14.8 41.5 %all_to_all.30 = bf16[48,4,768]{2,1,0:T(4,128)(2,1)} all-to-all(bf16[48,4,768]{2,1,0:T(4,128)(2,1)S(1)} %bitcast.62), channel_id=1, replica_groups=mesh['dp'=4,'expert'=48,'tensor'=4] {'expert'}, dimensions={0} | all-to-all | bytes 589824 | tf_op jit(solution)/shard_map/all_to_all | solution.py:50
  56.3 0.0 all-gather.5.cloned.1.call-start
  56.4 0.1 broadcast_in_dim.26
  56.5 23.4 %all_to_all.31 = bf16[48,4,768]{2,1,0:T(4,128)(2,1)} all-to-all(bf16[48,4,768]{2,1,0:T(4,128)(2,1)S(1)} %bitcast.63), channel_id=1, replica_groups=mesh['dp'=4,'expert'=48,'tensor'=4] {'expert'}, dimensions={0} | all-to-all | bytes 589824 | tf_op jit(solution)/shard_map/all_to_all | solution.py:50
  80.0 3.1 reshape.100
  83.1 2.9 fusion.9
  86.0 0.1 copy-done.13
  86.1 0.8 fusion.5
  86.9 0.8 convolution_convert_fusion
  87.7 1.1 copy.79
  88.8 4.0 all-to-all-start.1
  92.9 26.7 %all-gather.5.cloned.1.call-done = bf16[48,4,3072]{2,1,0:T(4,128)(2,1)} async-done(((bf16[48,4,768]{2,1,0:T(4,128)(2,1)}), bf16[48,4,3072]{2,1,0:T(4,128)(2,1)}) %all-gather.5.cloned.1.call-update) | async-done | bytes 1179664 | tf_op jit(solution)/shard_map/all_gather | solution.py:57
  119.6 3.1 reshape.107
  122.7 2.4 fusion.1
  125.1 1.0 fusion.7
  126.1 0.7 copy-done.4
  126.8 1.0 fusion
  127.8 1.1 copy.78
  128.9 4.3 all-to-all-start.4
  133.2 1.0 reduce_sum.97
  134.1 1.8 reshape.102
  135.9 13.4 %all-to-all-done.4 = bf16[4,192,768]{2,1,0:T(8,128)(2,1)} async-done(((bf16[4,192,768]{2,1,0:T(8,128)(2,1)}), bf16[4,192,768]{2,1,0:T(8,128)(2,1)}, u32[]{:S(2)}, u32[]{:S(2)}) %all-to-all-start.4) | async-done | bytes 1179680 | tf_op jit(solution)/shard_map/all_to_all | solution.py:16
  149.3 13.1 %all-to-all-start.2 = ((bf16[48,4,768]{2,1,0:T(4,128)(2,1)}), bf16[48,4,768]{2,1,0:T(4,128)(2,1)S(1)}, u32[]{:S(2)}, u32[]{:S(2)}) async-start(bf16[48,4,768]{2,1,0:T(4,128)(2,1)} %reshape.102), calls=%async_computation.2 | async-start | bytes 589824 | tf_op jit(solution)/shard_map/all_to_all | solution.py:64
  162.4 0.8 copy.64
  163.2 0.1 reshape.120
  163.3 1.5 reduce_sum.100
  164.8 0.8 reshape.109
  165.6 15.1 %all-to-all-done.2 = bf16[48,4,768]{2,1,0:T(4,128)(2,1)S(1)} async-done(((bf16[48,4,768]{2,1,0:T(4,128)(2,1)}), bf16[48,4,768]{2,1,0:T(4,128)(2,1)S(1)}, u32[]{:S(2)}, u32[]{:S(2)}) %all-to-all-start.2) | async-done | bytes 294944 | tf_op jit(solution)/shard_map/all_to_all | solution.py:64
  180.7 6.0 all-to-all-start.5
  186.8 0.0 all-reduce.2.cloned.1.call-start
  186.8 0.1 convert_reduce_fusion.1
  187.0 0.6 gather_fusion
  187.7 10.2 %all_gather.13 = bf16[16,2,3072]{2,0,1:T(8,128)(2,1)S(1)} all-gather(bf16[16,2,768]{2,0,1:T(8,128)(2,1)S(1)} %copy.65), channel_id=1, replica_groups=mesh['dp'=4,'expert'=48,'tensor'=4] {'tensor'}, dimensions={2}, use_global_device_ids=true | all-gather | bytes 245760 | tf_op jit(solution)/shard_map/all_gather | solution.py:75
  197.9 0.1 fusion.12
  198.1 2.1 fusion.34
  200.2 2.1 reshape.113
  202.3 2.6 all-to-all-done.5
  204.9 0.1 convert_reduce_fusion
  205.1 0.6 gather_fusion.1
  205.7 9.4 %all_gather.15 = bf16[16,2,3072]{2,1,0:T(2,128)(2,1)S(1)} all-gather(bf16[16,2,768]{2,1,0:T(2,128)(2,1)S(1)} %reshape.145), channel_id=1, replica_groups=mesh['dp'=4,'expert'=48,'tensor'=4] {'tensor'}, dimensions={2}, use_global_device_ids=true | all-gather | bytes 245760 | tf_op jit(solution)/shard_map/all_gather | solution.py:75
  215.1 0.5 convert_reduce_fusion.2
  215.7 0.5 fusion.23
  216.1 0.7 maximum_select_fusion
  216.8 0.8 fusion.20
  217.6 461.3 %all-reduce.2.cloned.1.call-done = f32[27648]{0:T(1024)} async-done(((f32[27648]{0:T(1024)}), f32[27648]{0:T(1024)}) %all-reduce.2.cloned.1.call-update) | async-done | bytes 110608 | tf_op jit(solution)/shard_map/psum | solution.py:25
  678.9 0.9 slice.49
  679.8 2.0 slice.41
  681.9 2.5 copy.70
  684.4 1.3 slice.50
  (59 shorter events, 0.4 us)
Async XLA Ops:
  7.2 79.7 %copy-start = (bf16[1,384,3072]{2,1,0:T(8,128)(2,1)S(1)}, bf16[1,384,3072]{2,1,0:T(8,128)(2,1)}, u32[]{:S(2)}) copy-start(bf16[1,384,3072]{2,1,0:T(8,128)(2,1)} %param.15) | copy-start | bytes 7077892
  7.2 72.8 %all-gather.3.cloned.1.call-start = ((), (), s32[]{:S(2)}) async-start(), calls=%async_computation.6 | async-start | bytes 1474560 | tf_op jit(solution)/shard_map/all_gather | solution.py:57
  12.0 1.9 copy-start.9
  13.0 0.9 copy-start.18
  13.0 0.9 copy-start.14
  14.0 69.1 %copy-start.6 = (f32[16,3072]{1,0:T(8,128)}, f32[16,3072]{1,0:T(8,128)S(1)}, u32[]{:S(2)}) copy-start(f32[16,3072]{1,0:T(8,128)S(1)} %convert_element_type.74) | copy-start | bytes 589828
  56.3 63.3 %all-gather.5.cloned.1.call-start = ((), (), s32[]{:S(2)}) async-start(), calls=%async_computation.7 | async-start | bytes 1474560 | tf_op jit(solution)/shard_map/all_gather | solution.py:57
  83.1 3.0 copy-start.3
  83.1 3.0 copy-start.13
  86.1 1.6 copy-start.1
  86.9 1.9 copy-start.11
  88.8 40.1 %all-to-all-start.1 = ((bf16[4,192,768]{2,1,0:T(8,128)(2,1)}), bf16[4,192,768]{2,1,0:T(8,128)(2,1)S(1)}, u32[]{:S(2)}, u32[]{:S(2)}) async-start(bf16[4,192,768]{2,1,0:T(8,128)(2,1)} %bitcast.57), calls=%async_computation.1 | async-start | bytes 2359296 | tf_op jit(solution)/shard_map/all_to_all | solution.py:16
  122.7 2.4 copy-start.2
  122.7 2.4 copy-start.5
  122.7 2.4 copy-start.12
  125.1 1.7 copy-start.4
  128.9 20.4 %all-to-all-start.4 = ((bf16[4,192,768]{2,1,0:T(8,128)(2,1)}), bf16[4,192,768]{2,1,0:T(8,128)(2,1)}, u32[]{:S(2)}, u32[]{:S(2)}) async-start(bf16[4,192,768]{2,1,0:T(8,128)(2,1)} %bitcast.58), calls=%async_computation.4 | async-start | bytes 2359296 | tf_op jit(solution)/shard_map/all_to_all | solution.py:16
  135.9 62.0 %copy-start.7 = (f32[16,3072]{1,0:T(8,128)S(1)}, f32[16,3072]{1,0:T(8,128)}, u32[]{:S(2)}) copy-start(f32[16,3072]{1,0:T(8,128)} %copy-done.6) | copy-start | bytes 589828
  149.3 31.4 %all-to-all-start.2 = ((bf16[48,4,768]{2,1,0:T(4,128)(2,1)}), bf16[48,4,768]{2,1,0:T(4,128)(2,1)S(1)}, u32[]{:S(2)}, u32[]{:S(2)}) async-start(bf16[48,4,768]{2,1,0:T(4,128)(2,1)} %reshape.102), calls=%async_computation.2 | async-start | bytes 589824 | tf_op jit(solution)/shard_map/all_to_all | solution.py:64
  162.4 35.6 %copy-start.10 = (bf16[16,3072]{1,0:T(8,128)(2,1)S(1)}, bf16[16,3072]{1,0:T(8,128)(2,1)}, u32[]{:S(2)}) copy-start(bf16[16,3072]{1,0:T(8,128)(2,1)} %copy-done.9) | copy-start | bytes 294916
  180.7 24.2 %all-to-all-start.5 = ((bf16[48,4,768]{2,1,0:T(4,128)(2,1)}), bf16[48,4,768]{2,1,0:T(4,128)(2,1)S(1)}, u32[]{:S(2)}, u32[]{:S(2)}) async-start(bf16[48,4,768]{2,1,0:T(4,128)(2,1)} %reshape.109), calls=%async_computation.5 | async-start | bytes 589824 | tf_op jit(solution)/shard_map/all_to_all | solution.py:64
  186.8 492.2 %all-reduce.2.cloned.1.call-start = ((), (), s32[]{:S(2)}) async-start(), calls=%async_computation.8 | async-start | bytes 221184 | tf_op jit(solution)/shard_map/psum | solution.py:25
  198.0 17.6 %copy-start.8 = (bf16[16,3072]{1,0:T(8,128)(2,1)S(1)}, bf16[16,3072]{1,0:T(8,128)(2,1)}, u32[]{:S(2)}) copy-start(bf16[16,3072]{1,0:T(8,128)(2,1)} %param.9) | copy-start | bytes 294916
  198.0 17.6 %copy-start.16 = (bf16[3072,8]{0,1:T(8,128)(2,1)S(1)}, bf16[3072,8]{0,1:T(8,128)(2,1)}, u32[]{:S(2)}) copy-start(bf16[3072,8]{0,1:T(8,128)(2,1)} %param.12) | copy-start | bytes 147460
  198.1 17.6 %copy-start.17 = (f32[3072]{0:T(1024)S(1)}, f32[3072]{0:T(1024)}, u32[]{:S(2)}) copy-start(f32[3072]{0:T(1024)} %param.11) | copy-start | bytes 36868
  200.2 16.6 %copy-start.15 = (bf16[16,3072]{1,0:T(8,128)(2,1)S(1)}, bf16[16,3072]{1,0:T(8,128)(2,1)}, u32[]{:S(2)}) copy-start(bf16[16,3072]{1,0:T(8,128)(2,1)} %param.10) | copy-start | bytes 294916
  200.2 16.6 %copy-start.19 = (f32[16]{0:T(128)S(1)}, f32[16]{0:T(128)}, u32[]{:S(2)}) copy-start(f32[16]{0:T(128)} %get-tuple-element.32) | copy-start | bytes 196
Sparse Core Ops, SparseCore 0:
  56.4 22.7 all-gather.2
  81.7 37.8 all-gather.4
  216.9 461.9 all-reduce.1

commit v2 on v0

v2 whole, which is shorter than its diff:
```python
import functools

import jax
import jax.numpy as jnp
from jax import lax
from jax.experimental import pallas as pl
from jax.experimental.pallas import tpu as pltpu
from jax.sharding import PartitionSpec as P

epsilon = 1e-05
LANES = 128
SLOTS = 4
LINE = 4
F32 = jnp.float32
BF16 = jnp.bfloat16
NT = (((1,), (1,)), ((), ()))


def low_rows(shape):
    return lax.broadcasted_iota(jnp.int32, shape, 1) < SLOTS


def split_rows(tiles):
    n = tiles.shape[0]
    pairs = tiles.reshape(n // 2, 2, 8, LANES)
    a, b = pairs[:, 0], pairs[:, 1]
    low = low_rows(a.shape)
    first = jnp.where(low, a, pltpu.roll(b, SLOTS, 1))
    second = jnp.where(low, pltpu.roll(a, SLOTS, 1), b)
    return first.reshape(4 * n, LANES), second.reshape(4 * n, LANES)


def join_rows(first, second):
    n = first.shape[0] // 4
    first = first.reshape(n // 2, 8, LANES)
    second = second.reshape(n // 2, 8, LANES)
    low = low_rows(first.shape)
    a = jnp.where(low, first, pltpu.roll(second, SLOTS, 1))
    b = jnp.where(low, pltpu.roll(first, SLOTS, 1), second)
    return jnp.concatenate([a[:, None], b[:, None]], axis=1).reshape(n, 8, LANES)


def layer_kernel(
    dims,
    tokens_ref, cot_ref, gain_ref, router_ref, sel0_ref, sel1_ref, selT0_ref, selT1_ref, sign_ref,
    gate_hbm, up_hbm, down_hbm,
    mixed_ref, gtok_ref, grouter_ref, ggain_ref,
    wg, wu, wd, packed, arrived, xin, gin, pre, hid, parts, fwd_in, left_in, right_in, reduced,
    copy_in, finished, back, mixed_all, gtok_all, scal_out, scal_in, sums, line_in, line_sum,
    z_in, z_sum, grads,
    w_sem, a2a_sem, cp_send, cp_recv, xl_send, xr_send, xf_send, xl_recv, xr_recv, xf_recv,
    f_send, f_recv, l_send, r_send, l_recv, r_recv, c_send, c_recv, back_sem,
    sc_send, sc_recv, mx_send, mx_recv, gt_send, gt_recv, line_sem, z_sem, gl_sem, gx_send, gx_recv,
):
    n_dp, n_e, n_t, experts, copies = dims
    width = copies * LANES
    half = copies // 2
    d, e, t = lax.axis_index("dp"), lax.axis_index("expert"), lax.axis_index("tensor")
    k, s = e // copies, e % copies
    z, line = e // LINE, d * LINE + e % LINE
    n_z, n_line = n_e // LINE, n_dp * LINE
    left, right, across = (t + n_t - 1) % n_t, (t + 1) % n_t, (t + 2) % n_t
    mine = t * copies + s
    sl = pl.ds(pl.multiple_of(t * width, LANES), width)

    def place(dp, expert, tensor):
        return (dp, expert, tensor)

    def remote(src, dst, send, recv, target):
        return pltpu.make_async_remote_copy(
            src_ref=src, dst_ref=dst, send_sem=send, recv_sem=recv,
            device_id=target, device_id_type=pl.DeviceIdType.MESH,
        )

    weights = [
        pltpu.make_async_copy(a, b, w_sem.at[i])
        for i, (a, b) in enumerate(((gate_hbm, wg), (up_hbm, wu), (down_hbm, wd)))
    ]
    for w in weights:
        w.start()

    bar = pltpu.get_barrier_semaphore()

    @pl.loop(1, n_e)
    def _(i):
        pl.semaphore_signal(bar, inc=1, device_id=place(d, (e + i) % n_e, t),
                            device_id_type=pl.DeviceIdType.MESH)

    for o in range(1, n_t):
        pl.semaphore_signal(bar, inc=1, device_id=place(d, e, (t + o) % n_t),
                            device_id_type=pl.DeviceIdType.MESH)

    @pl.loop(0, (n_dp - 1) * LINE)
    def _(i):
        pl.semaphore_signal(
            bar, inc=1, device_id=place((d + 1 + i // LINE) % n_dp, z * LINE + i % LINE, t),
            device_id_type=pl.DeviceIdType.MESH)

    floats = tokens_ref[...].astype(F32)
    inv_rms = lax.rsqrt(jnp.mean(floats * floats, axis=1, keepdims=True) + epsilon)
    normed = (floats * inv_rms * gain_ref[...]).astype(BF16)
    logits = lax.dot_general(normed, router_ref[...], NT, preferred_element_type=F32)
    sign = sign_ref[...]
    p0 = jax.nn.sigmoid(jnp.sum(logits * sign, axis=1, keepdims=True))
    p1 = 1.0 - p0
    toks = tokens_ref[:, sl].astype(F32)
    cots = cot_ref[:, sl].astype(F32)
    gains = gain_ref[:, sl]
    normeds = (toks * inv_rms * gains).astype(BF16)
    selT0, selT1 = selT0_ref[...], selT1_ref[...]
    rows_in = jnp.dot(selT0 + selT1, normeds, preferred_element_type=F32)
    rows_g = (jnp.dot(selT0, (p0 * cots).astype(BF16), preferred_element_type=F32)
              + jnp.dot(selT1, (p1 * cots).astype(BF16), preferred_element_type=F32))
    for c in range(copies):
        at = slice(c * LANES, (c + 1) * LANES)
        packed[:, c] = join_rows(rows_in[:, at], rows_g[:, at]).astype(BF16)

    pl.semaphore_wait(bar, n_e - 1 + n_t - 1 + (n_dp - 1) * LINE)

    @pl.loop(1, n_e)
    def _(i):
        to = (e + i) % n_e
        remote(packed.at[to // copies, to % copies], arrived.at[t * copies + to % copies, e],
               a2a_sem.at[0], a2a_sem.at[1], place(d, to, t)).start()

    arrived[mine, e] = packed[k, s]
    scaled = floats * gain_ref[...]
    router = router_ref[...].astype(F32)
    through = jnp.concatenate(
        [jnp.sum(scaled * router[j : j + 1], axis=1, keepdims=True) for j in range(experts)], axis=1)

    a2a = remote(arrived.at[mine, pl.ds(0, n_e - 1)], arrived.at[mine, pl.ds(0, n_e - 1)],
                 a2a_sem.at[0], a2a_sem.at[1], place(d, e, right))
    a2a.wait_recv()

    def piece(i):
        return (s + i) % copies

    started = []

    def go(copy):
        copy.start()
        started.append(copy)

    for i in range(1, copies):
        go(remote(arrived.at[mine], arrived.at[mine], cp_send.at[i], cp_recv.at[s],
                  place(d, k * copies + piece(i), t)))

    def chunk(tensor, i):
        return arrived.at[tensor * copies + piece(i)]

    def from_left(i):
        remote(chunk(left, i), chunk(left, i), xr_send.at[i], xr_recv.at[i], place(d, e, right)).wait_recv()

    def from_right(i):
        remote(chunk(right, i), chunk(right, i), xl_send.at[i], xl_recv.at[i], place(d, e, left)).wait_recv()

    def pass_on(i):
        from_left(i)
        from_right(i)
        if i < half:
            go(remote(chunk(left, i), chunk(left, i), xf_send.at[i], xf_recv.at[i], place(d, e, right)))
        else:
            go(remote(chunk(right, i), chunk(right, i), xf_send.at[i], xf_recv.at[i], place(d, e, left)))

    for i in range(copies):
        if i > 0:
            remote(chunk(t, i), chunk(t, i), cp_send.at[i], cp_recv.at[piece(i)], place(d, e, right)).wait_recv()
        go(remote(chunk(t, i), chunk(t, i), xr_send.at[i], xr_recv.at[i], place(d, e, right)))
        go(remote(chunk(t, i), chunk(t, i), xl_send.at[i], xl_recv.at[i], place(d, e, left)))
        if i > 0:
            pass_on(i - 1)
    pass_on(copies - 1)

    pre[...] = jnp.zeros_like(pre)
    for w in weights:
        w.wait()

    def features(q):
        for c in range(copies):
            first, second = split_rows(arrived[q * copies + c].astype(F32))
            at = slice(c * LANES, (c + 1) * LANES)
            xin[:, at] = first.astype(BF16)
            gin[:, at] = second.astype(BF16)
        x, g = xin[...], gin[...]
        pre[0] += jnp.dot(x, wg[q], preferred_element_type=F32)
        pre[1] += jnp.dot(x, wu[q], preferred_element_type=F32)
        down = wd[:, pl.ds(pl.multiple_of(q * width, LANES), width)]
        pre[2] += lax.dot_general(g, down, NT, preferred_element_type=F32)

    @pl.loop(0, n_t - 1)
    def _(j):
        features((t + jnp.where(j == 2, 3, j)) % n_t)

    for i in range(copies):
        remote(chunk(across, i), chunk(across, i), xf_send.at[i], xf_recv.at[i],
               place(d, e, right)).wait_recv()
    features(across)

    gate, up, grad_act = pre[0], pre[1], pre[2]
    sig = jax.nn.sigmoid(gate)
    silu = gate * sig
    hid[0] = (silu * up).astype(BF16)
    hid[1] = (grad_act * up * sig * (1.0 + gate * (1.0 - sig))).astype(BF16)
    hid[2] = (grad_act * silu).astype(BF16)

    def quarter(q):
        down = wd[:, pl.ds(pl.multiple_of(q * width, LANES), width)]
        y = jnp.dot(hid[0], down, preferred_element_type=F32)
        g = (lax.dot_general(hid[1], wg[q], NT, preferred_element_type=F32)
             + lax.dot_general(hid[2], wu[q], NT, preferred_element_type=F32))
        for c in range(copies):
            at = slice(c * LANES, (c + 1) * LANES)
            parts[q, c] = join_rows(y[:, at], g[:, at]).astype(BF16)

    order = [(i + 1) % copies for i in range(copies)]
    quarter(across)
    for i in order:
        src = parts.at[across, piece(i)]
        go(remote(src, fwd_in.at[i], f_send.at[i], f_recv.at[i], place(d, e, right if i < half else left)))

    @pl.loop(0, 3)
    def _(j):
        quarter((t + jnp.where(j == 0, 1, jnp.where(j == 1, n_t - 1, 0))) % n_t)

    for i in order:
        remote(fwd_in.at[i], fwd_in.at[i], f_send.at[i], f_recv.at[i], place(d, e, right)).wait_recv()
        on = right if i < half else left
        parts[on, piece(i)] = (parts[on, piece(i)].astype(F32) + fwd_in[i].astype(F32)).astype(BF16)
        go(remote(parts.at[right, piece(i)], left_in.at[i], r_send.at[i], r_recv.at[i], place(d, e, right)))
        go(remote(parts.at[left, piece(i)], right_in.at[i], l_send.at[i], l_recv.at[i], place(d, e, left)))

    for i in order:
        remote(left_in.at[i], left_in.at[i], r_send.at[i], r_recv.at[i], place(d, e, right)).wait_recv()
        remote(right_in.at[i], right_in.at[i], l_send.at[i], l_recv.at[i], place(d, e, left)).wait_recv()
        total = parts[t, piece(i)].astype(F32) + left_in[i].astype(F32) + right_in[i].astype(F32)
        reduced[i] = total.astype(BF16)
        if i > 0:
            go(remote(reduced.at[i], copy_in.at[i], c_send.at[i], c_recv.at[i],
                      place(d, k * copies + piece(i), t)))
    total = reduced[0].astype(F32)
    for i in range(1, copies):
        remote(copy_in.at[i], copy_in.at[i], c_send.at[i], c_recv.at[i], place(d, e, right)).wait_recv()
        total = total + copy_in[i].astype(F32)
    finished[...] = total.astype(BF16)

    @pl.loop(1, n_e)
    def _(i):
        to = (e + i) % n_e
        remote(finished.at[to], back.at[k, s], back_sem.at[0], back_sem.at[1], place(d, to, t)).start()

    back[k, s] = finished[e]
    bulk = arrived.at[0, pl.ds(0, n_e - 1)]
    back_bulk = remote(bulk, bulk, back_sem.at[0], back_sem.at[1], place(d, e, right))
    back_bulk.wait_recv()

    ys, gs = [], []
    for c in range(copies):
        first, second = split_rows(back[:, c].astype(F32))
        ys.append(first.astype(BF16))
        gs.append(second.astype(BF16))
    y, g = jnp.concatenate(ys, axis=1), jnp.concatenate(gs, axis=1)
    sel0, sel1 = sel0_ref[...], sel1_ref[...]
    chosen0 = jnp.dot(sel0, y, preferred_element_type=F32)
    chosen1 = jnp.dot(sel1, y, preferred_element_type=F32)
    grad_mix = jnp.dot(sel0 + sel1, g, preferred_element_type=F32)
    rows = toks.shape[0]
    diff = jnp.sum(cots * (chosen0 - chosen1), axis=1, keepdims=True)
    dots = jnp.sum(grad_mix * gains * toks, axis=1, keepdims=True)
    column = lax.broadcasted_iota(jnp.int32, (rows, LANES), 1)
    scal_out[...] = jnp.where(column == 0, diff, jnp.where(column == 1, dots, 0.0))
    mixed_all[t] = (toks + (p0 * chosen0 + p1 * chosen1)).astype(BF16)
    for o in range(1, n_t):
        go(remote(scal_out, scal_in.at[o - 1], sc_send.at[o - 1], sc_recv.at[o - 1], place(d, e, (t + o) % n_t)))
    for o in range(1, n_t):
        go(remote(mixed_all.at[t], mixed_all.at[t], mx_send.at[o - 1], mx_recv.at[o - 1],
                  place(d, e, (t + o) % n_t)))
    scalars = scal_out[...]
    for o in range(1, n_t):
        remote(scal_in.at[o - 1], scal_in.at[o - 1], sc_send.at[o - 1], sc_recv.at[o - 1],
               place(d, e, right)).wait_recv()
        scalars = scalars + scal_in[o - 1]
    grad_first = p0 * p1 * scalars[:, 0:1]
    grad_logits = grad_first * sign
    grad_normed = grad_mix
    routers = router_ref[:, sl].astype(F32)
    for j in range(experts):
        grad_normed = grad_normed + grad_logits[:, j : j + 1] * routers[j : j + 1]
    normed32 = normeds.astype(F32)
    router_part = jnp.concatenate(
        [jnp.sum(grad_logits[:, j : j + 1] * normed32, axis=0, keepdims=True) for j in range(experts)], axis=0)
    gain_part = jnp.sum(grad_normed * toks * inv_rms, axis=0, keepdims=True)
    units = sums.shape[1]

    def unit(u):
        return u // units, u % units

    n_half = experts // SLOTS
    for c in range(copies):
        at = slice(c * LANES, (c + 1) * LANES)
        for h in range(n_half):
            a, b = unit(c * n_half + h)
            sums[a, b] = router_part[h * SLOTS : (h + 1) * SLOTS, at]
        a, b = unit(n_half * copies + c // SLOTS)
        sums[a, b, c % SLOTS : c % SLOTS + 1] = gain_part[:, at]

    def member(i):
        j = (line + i) % n_line
        return j, place(j // LINE, z * LINE + j % LINE, t)

    @pl.loop(1, n_line)
    def _(i):
        j, target = member(i)
        remote(sums.at[j], line_in.at[line], line_sem.at[0], line_sem.at[1], target).start()

    mean = (scalars[:, 1:2] + jnp.sum(grad_logits * through, axis=1, keepdims=True)) / (n_t * width)
    cubed = inv_rms * inv_rms * inv_rms
    gtok_all[t] = (cots + inv_rms * (grad_normed * gains) - toks * cubed * mean).astype(BF16)
    for o in range(1, n_t):
        go(remote(gtok_all.at[t], gtok_all.at[t], gt_send.at[o - 1], gt_recv.at[o - 1],
                  place(d, e, (t + o) % n_t)))
    line_in[line] = sums[line]
    some = pl.ds(0, n_line - 1)
    line_bulk = remote(line_in.at[some], line_in.at[some], line_sem.at[0], line_sem.at[1], place(d, e, right))
    line_bulk.wait_recv()
    line_sum[...] = jnp.sum(line_in[...], axis=0)

    if n_z > 1:
        @pl.loop(1, n_z)
        def _(i):
            to = (z + i) % n_z
            remote(line_sum, z_in.at[z], z_sem.at[0], z_sem.at[1], place(d, to * LINE + e % LINE, t)).start()

        z_in[z] = line_sum[...]
        zs = pl.ds(0, n_z - 1)
        z_bulk = remote(z_in.at[zs], z_in.at[zs], z_sem.at[0], z_sem.at[1], place(d, e, right))
        z_bulk.wait_recv()
        z_sum[...] = jnp.sum(z_in[...], axis=0)
    else:
        z_sum[...] = line_sum[...]

    @pl.loop(1, n_line)
    def _(i):
        j, target = member(i)
        remote(z_sum, grads.at[t, line], gl_sem.at[0], gl_sem.at[1], target).start()

    grads[t, line] = z_sum[...]
    gl_bulk = remote(grads.at[t, some], grads.at[t, some], gl_sem.at[0], gl_sem.at[1], place(d, e, right))
    gl_bulk.wait_recv()
    for o in range(1, n_t):
        go(remote(grads.at[t], grads.at[t], gx_send.at[o - 1], gx_recv.at[o - 1], place(d, e, (t + o) % n_t)))

    def other(o):
        return (t + n_t - o) % n_t

    for o in range(1, n_t):
        remote(mixed_all.at[other(o)], mixed_all.at[other(o)], mx_send.at[o - 1], mx_recv.at[o - 1],
               place(d, e, right)).wait_recv()
        remote(gtok_all.at[other(o)], gtok_all.at[other(o)], gt_send.at[o - 1], gt_recv.at[o - 1],
               place(d, e, right)).wait_recv()
    for q in range(n_t):
        at = slice(q * width, (q + 1) * width)
        mixed_ref[:, at] = mixed_all[q]
        gtok_ref[:, at] = gtok_all[q]
    for o in range(1, n_t):
        remote(grads.at[other(o)], grads.at[other(o)], gx_send.at[o - 1], gx_recv.at[o - 1],
               place(d, e, right)).wait_recv()
    for q in range(n_t):
        for c in range(copies):
            at = slice(q * width + c * LANES, q * width + (c + 1) * LANES)
            for h in range(n_half):
                a, b = unit(c * n_half + h)
                grouter_ref[h * SLOTS : (h + 1) * SLOTS, at] = grads[q, a, b]
            a, b = unit(n_half * copies + c // SLOTS)
            ggain_ref[:, at] = grads[q, a, b, c % SLOTS : c % SLOTS + 1]

    a2a.wait_send()
    back_bulk.wait_send()
    line_bulk.wait_send()
    if n_z > 1:
        z_bulk.wait_send()
    gl_bulk.wait_send()
    for copy in started:
        copy.wait_send()


def shards(dims, tokens, cotangent, gain, w_router, w_gate, w_up, w_down, expert_ids, slots):
    n_dp, n_e, n_t, experts, copies = dims
    count, features = tokens.shape
    hidden = w_gate.shape[2]
    width = features // n_t
    n_rows = n_e * SLOTS
    n_line, n_z = n_dp * LINE, n_e // LINE
    row_index = expert_ids * SLOTS + slots
    tile = jnp.arange(experts * SLOTS, dtype=jnp.int32)
    sel = [(row_index[:, c : c + 1] == tile[None, :]).astype(BF16) for c in range(2)]
    sel_t = [(row_index[:, c][None, :] == tile[:, None]).astype(BF16) for c in range(2)]
    columns = jnp.arange(experts, dtype=jnp.int32)[None, :]
    sign = (expert_ids[:, 0:1] == columns).astype(F32) - (expert_ids[:, 1:2] == columns).astype(F32)
    units = -(-(copies * (experts // SLOTS) + -(-copies // SLOTS)) // n_line)
    block = (n_e, 8, LANES)
    dma = pltpu.SemaphoreType.DMA
    vmem = pl.BlockSpec(memory_space=pltpu.VMEM)
    scratch = [
        pltpu.VMEM((n_t, width, hidden), BF16), pltpu.VMEM((n_t, width, hidden), BF16),
        pltpu.VMEM((hidden, features), BF16),
        pltpu.VMEM((experts, copies, 8, LANES), BF16),
        pltpu.VMEM((n_t * copies,) + block, BF16),
        pltpu.VMEM((n_rows, width), BF16), pltpu.VMEM((n_rows, width), BF16),
        pltpu.VMEM((3, n_rows, hidden), F32), pltpu.VMEM((3, n_rows, hidden), BF16),
        pltpu.VMEM((n_t, copies) + block, BF16),
        pltpu.VMEM((copies,) + block, BF16), pltpu.VMEM((copies,) + block, BF16),
        pltpu.VMEM((copies,) + block, BF16), pltpu.VMEM((copies,) + block, BF16),
        pltpu.VMEM((copies,) + block, BF16),
        pltpu.VMEM(block, BF16),
        pltpu.VMEM((experts, copies, 8, LANES), BF16),
        pltpu.VMEM((n_t, count, width), BF16), pltpu.VMEM((n_t, count, width), BF16),
        pltpu.VMEM((count, LANES), F32), pltpu.VMEM((n_t - 1, count, LANES), F32),
        pltpu.VMEM((n_line, units, SLOTS, LANES), F32), pltpu.VMEM((n_line, units, SLOTS, LANES), F32),
        pltpu.VMEM((units, SLOTS, LANES), F32),
        pltpu.VMEM((n_z, units, SLOTS, LANES), F32), pltpu.VMEM((units, SLOTS, LANES), F32),
        pltpu.VMEM((n_t, n_line, units, SLOTS, LANES), F32),
        dma((3,)), dma((2,)),
    ] + [dma((copies,))] * 16 + [dma((2,))] + [dma((n_t - 1,))] * 6 + [dma((2,))] * 3 + [dma((n_t - 1,))] * 2
    mixed, gtok, grouter, ggain = pl.pallas_call(
        functools.partial(layer_kernel, dims),
        out_shape=(
            jax.ShapeDtypeStruct((count, features), BF16), jax.ShapeDtypeStruct((count, features), BF16),
            jax.ShapeDtypeStruct((experts, features), F32), jax.ShapeDtypeStruct((1, features), F32),
        ),
        in_specs=[vmem] * 9 + [pl.BlockSpec(memory_space=pl.ANY)] * 3,
        out_specs=(vmem,) * 4,
        scratch_shapes=scratch,
        compiler_params=pltpu.CompilerParams(
            collective_id=0, has_side_effects=True, vmem_limit_bytes=56 * 1024 * 1024),
    )(
        tokens, cotangent, gain.reshape(1, features), w_router.T, sel[0], sel[1], sel_t[0], sel_t[1], sign,
        w_gate.reshape(n_t, width, hidden), w_up.reshape(n_t, width, hidden), w_down.reshape(hidden, features),
    )
    return mixed, gtok, grouter.T, ggain.reshape(features)


def solution(mesh):
    n_dp, n_e, n_t = (mesh.shape[a] for a in ("dp", "expert", "tensor"))

    def body(*args):
        experts = args[3].shape[1]
        return shards((n_dp, n_e, n_t, experts, n_e // experts), *args)

    return jax.shard_map(
        body,
        mesh=mesh,
        in_specs=(
            P(("dp", "expert"), None),
            P(("dp", "expert"), None),
            P(),
            P(),
            P("expert", None, "tensor"),
            P("expert", None, "tensor"),
            P("expert", "tensor", None),
            P(("dp", "expert"), None),
            P(("dp", "expert"), None),
        ),
        out_specs=(P(("dp", "expert"), None), P(("dp", "expert"), None), P(), P()),
        check_vma=False,
    )
```

time: 527 us -> 143 us (0.27)
  waiting for transfers between devices: 348 us -> 0 us
  Pallas kernels: 0 us -> 133 us
  blocking collectives: 84.6 us -> 0 us
  starting transfers between devices: 27.1 us -> 0 us
  local copies, waits for them, and re-layouts: 25.3 us -> 6.69 us
  matrix products: 14.8 us -> 0 us
  between operations: 14.2 us -> 0.64 us
  other arithmetic: 11.6 us -> 2.64 us
    psum x1 -> x0, waiting for transfers between devices: 273 us -> none  [in_one(): so_far = lax.psum(line, axis)]
    pallas_call x0 -> x1, Pallas kernels: none -> 133 us  [shards(): pl.pallas_call(functools.partial(layer_kernel, dims), out_shape=(jax.Shap...]
    all_to_all x2 -> x0, blocking collectives: 64.9 us -> none  [to_experts(): lax.all_to_all(repeat_blocks(feature_slice, experts, copies), 'expert', s...]
    all_to_all x4 -> x0, waiting for transfers between devices: 47.5 us -> none  [the longest x2 34.4 us: from_experts(): lax.all_to_all(partial_value.reshape(experts * copies, -1, feature_width)...]
    all_to_all x4 -> x0, starting transfers between devices: 27 us -> none  [the longest x2 18.7 us: from_experts(): lax.all_to_all(partial_value.reshape(experts * copies, -1, feature_width)...]
    all_gather x2 -> x0, waiting for transfers between devices: 26.8 us -> none  [to_experts(): arrived = lax.all_gather(arrived, 'tensor', axis=2, tiled=True)]
    all_gather x2 -> x0, blocking collectives: 19.7 us -> none  [from_experts(): lax.all_gather(picked.astype(jnp.bfloat16), 'tensor', axis=2, tiled=True)]
    dot_general x11 -> x0, matrix products: 14.8 us -> none  [the longest x1 3.03 us: shards(): jnp.dot(normed.astype(jnp.float32).T, grad_logits, precision=lax.Precisio...]
  transfers between devices with their start and end apart: 7 -> 0, of which waited for: 5 -> 0; matrix products, arithmetic and copies ran while one was open for 6% -> 0% of each run, Pallas kernels for 0% -> 0%
where the time goes in v2:
time: 143 us
  Pallas kernels  133 us (93%)
  local copies, waits for them, and re-layouts  6.69 us (5%)
  other arithmetic  2.64 us (2%)
    pallas_call x1, Pallas kernels, shards(): pl.pallas_call(functools.partial(layer_kernel, dims), out_shape=(jax.Shap...  133 us
    unnamed x4, local copies, waits for them, and re-layouts  5.92 us

profile of v2, /device:TPU:1, one launch (start us, length us, event | category | flops | bytes accessed | tf_op | source)
XLA Modules:
  0.0 143.1 jit_solution(9676874476431952196)
XLA Ops:
  0.6 0.7 multiply_add_fusion
  1.3 0.8 slice_bitcast_fusion.1
  2.1 0.7 convert_subtract_fusion.sign_ref
  2.8 0.7 fusion.2
  3.4 0.6 fusion
  4.0 133.1 %shard_map.120 = (bf16[16,3072]{1,0:T(8,128)(2,1)}, bf16[16,3072]{1,0:T(8,128)(2,1)}, f32[8,3072]{1,0:T(8,128)}, f32[1,3072]{1,0:T(1,128)}) custom-call(bf16[16,3072]{1,0:T(8,128)(2,1)} %tokens_ref.1, bf16[16,3072]{1,0:T(8,128)(2,1)} %cot_ref.1, f32[1,3072]{1,0:T(1,128)} %bitcast.21, bf16[8,3072]{1,0:T(8,128)(2,1)} %bitcast.19, ...), custom_call_target="tpu_custom_call" | custom-call | tf_op jit(solution)/shard_map/pallas_call | solution.py:425
  137.2 1.5 %copy.17 = bf16[16,3072]{1,0:T(8,128)(2,1)} copy(bf16[16,3072]{1,0:T(8,128)(2,1)} %get-tuple-element.24) | data formatting | bytes 196608
  138.7 1.5 %copy.18 = bf16[16,3072]{1,0:T(8,128)(2,1)} copy(bf16[16,3072]{1,0:T(8,128)(2,1)} %get-tuple-element.25) | data formatting | bytes 196608
  140.3 1.5 %copy.19 = f32[3072,8]{0,1:T(8,128)} copy(f32[3072,8]{0,1:T(8,128)} %bitcast.18) | data formatting | bytes 196608
  141.8 1.3 copy.20
  (1 shorter events, 0.0 us)

commit v3 on v2

--- a/solution.py
+++ b/solution.py
@@ -11,6 +11,9 @@
 LANES = 128
 SLOTS = 4
 LINE = 4
+BANDS = 3
+LAG = 3
+AHEAD = 2
 F32 = jnp.float32
 BF16 = jnp.bfloat16
 NT = (((1,), (1,)), ((), ()))
@@ -40,14 +43,31 @@
     return jnp.concatenate([a[:, None], b[:, None]], axis=1).reshape(n, 8, LANES)
 
 
+def one_hots(ids, slots, experts):
+    count, n_rows = ids.shape[1], experts * SLOTS
+    rows = ids * SLOTS + slots
+    at = lax.broadcasted_iota(jnp.int32, (n_rows, count), 0)
+    picks = [(at == rows[c : c + 1]).astype(F32) for c in range(2)]
+    expert = lax.broadcasted_iota(jnp.int32, (experts, count), 0)
+    signs = (expert == ids[0:1]).astype(F32) - (expert == ids[1:2]).astype(F32)
+    both = jnp.concatenate(picks + [signs], axis=0)
+    fill = -both.shape[0] % LANES
+    both = jnp.concatenate([both, jnp.zeros((fill, count), F32)], axis=0)
+    both = jnp.concatenate([both, jnp.zeros((both.shape[0], LANES - count), F32)], axis=1)
+    turned = both.T
+    sel0 = turned[:count, :n_rows].astype(BF16)
+    sel1 = turned[:count, n_rows : 2 * n_rows].astype(BF16)
+    sign = turned[:count, 2 * n_rows : 2 * n_rows + experts]
+    return sel0, sel1, sign, picks[0].astype(BF16), picks[1].astype(BF16)
+
+
 def layer_kernel(
     dims,
-    tokens_ref, cot_ref, gain_ref, router_ref, sel0_ref, sel1_ref, selT0_ref, selT1_ref, sign_ref,
+    tokens_ref, cot_ref, gain_ref, router_ref, ids_ref, slots_ref,
     gate_hbm, up_hbm, down_hbm,
-    mixed_ref, gtok_ref, grouter_ref, ggain_ref,
+    mixed_all, gtok_all, grads,
     wg, wu, wd, packed, arrived, xin, gin, pre, hid, parts, fwd_in, left_in, right_in, reduced,
-    copy_in, finished, back, mixed_all, gtok_all, scal_out, scal_in, sums, line_in, line_sum,
-    z_in, z_sum, grads,
+    copy_in, finished, back, scal_out, scal_in, sums, line_in, line_sum, z_in, z_sum,
     w_sem, a2a_sem, cp_send, cp_recv, xl_send, xr_send, xf_send, xl_recv, xr_recv, xf_recv,
     f_send, f_recv, l_send, r_send, l_recv, r_recv, c_send, c_recv, back_sem,
     sc_send, sc_recv, mx_send, mx_recv, gt_send, gt_recv, line_sem, z_sem, gl_sem, gx_send, gx_recv,
@@ -100,14 +120,13 @@
     inv_rms = lax.rsqrt(jnp.mean(floats * floats, axis=1, keepdims=True) + epsilon)
     normed = (floats * inv_rms * gain_ref[...]).astype(BF16)
     logits = lax.dot_general(normed, router_ref[...], NT, preferred_element_type=F32)
-    sign = sign_ref[...]
+    sel0, sel1, sign, selT0, selT1 = one_hots(ids_ref[...], slots_ref[...], experts)
     p0 = jax.nn.sigmoid(jnp.sum(logits * sign, axis=1, keepdims=True))
     p1 = 1.0 - p0
     toks = tokens_ref[:, sl].astype(F32)
     cots = cot_ref[:, sl].astype(F32)
     gains = gain_ref[:, sl]
     normeds = (toks * inv_rms * gains).astype(BF16)
-    selT0, selT1 = selT0_ref[...], selT1_ref[...]
     rows_in = jnp.dot(selT0 + selT1, normeds, preferred_element_type=F32)
     rows_g = (jnp.dot(selT0, (p0 * cots).astype(BF16), preferred_element_type=F32)
               + jnp.dot(selT1, (p1 * cots).astype(BF16), preferred_element_type=F32))
@@ -142,35 +161,46 @@
         copy.start()
         started.append(copy)
 
-    for i in range(1, copies):
-        go(remote(arrived.at[mine], arrived.at[mine], cp_send.at[i], cp_recv.at[s],
-                  place(d, k * copies + piece(i), t)))
-
-    def chunk(tensor, i):
-        return arrived.at[tensor * copies + piece(i)]
-
-    def from_left(i):
-        remote(chunk(left, i), chunk(left, i), xr_send.at[i], xr_recv.at[i], place(d, e, right)).wait_recv()
-
-    def from_right(i):
-        remote(chunk(right, i), chunk(right, i), xl_send.at[i], xl_recv.at[i], place(d, e, left)).wait_recv()
-
-    def pass_on(i):
-        from_left(i)
-        from_right(i)
-        if i < half:
-            go(remote(chunk(left, i), chunk(left, i), xf_send.at[i], xf_recv.at[i], place(d, e, right)))
-        else:
-            go(remote(chunk(right, i), chunk(right, i), xf_send.at[i], xf_recv.at[i], place(d, e, left)))
-
-    for i in range(copies):
+    bands = cp_send.shape[1]
+    span = n_e // bands
+
+    def band(tensor, i, h):
+        return arrived.at[tensor * copies + piece(i), pl.ds(h * span, span)]
+
+    def arrives(block, recv):
+        remote(block, block, cp_send.at[0, 0], recv, place(d, e, right)).wait_recv()
+
+    def to_copies(h):
+        for i in range(1, copies):
+            own = band(t, 0, h)
+            go(remote(own, own, cp_send.at[i, h], cp_recv.at[s, h], place(d, k * copies + piece(copies - i), t)))
+
+    to_copies(0)
+
+    def both_ways(i, h):
+        block = band(t, i, h)
+        go(remote(block, block, xr_send.at[i, h], xr_recv.at[i, h], place(d, e, right)))
+        go(remote(block, block, xl_send.at[i, h], xl_recv.at[i, h], place(d, e, left)))
+
+    def pass_on(i, h):
+        arrives(band(left, i, h), xr_recv.at[i, h])
+        arrives(band(right, i, h), xl_recv.at[i, h])
+        block, to = (band(left, i, h), right) if i < half else (band(right, i, h), left)
+        go(remote(block, block, xf_send.at[i, h], xf_recv.at[i, h], place(d, e, to)))
+
+    steps = [(i, h) for h in range(bands) for i in range(copies)]
+    waiting = []
+    for i, h in steps:
         if i > 0:
-            remote(chunk(t, i), chunk(t, i), cp_send.at[i], cp_recv.at[piece(i)], place(d, e, right)).wait_recv()
-        go(remote(chunk(t, i), chunk(t, i), xr_send.at[i], xr_recv.at[i], place(d, e, right)))
-        go(remote(chunk(t, i), chunk(t, i), xl_send.at[i], xl_recv.at[i], place(d, e, left)))
-        if i > 0:
-            pass_on(i - 1)
-    pass_on(copies - 1)
+            arrives(band(t, i, h), cp_recv.at[piece(i), h])
+        both_ways(i, h)
+        if i == AHEAD and h + 1 < bands:
+            to_copies(h + 1)
+        waiting.append((i, h))
+        if len(waiting) > LAG:
+            pass_on(*waiting.pop(0))
+    for i, h in waiting:
+        pass_on(i, h)
 
     pre[...] = jnp.zeros_like(pre)
     for w in weights:
@@ -192,9 +222,8 @@
     def _(j):
         features((t + jnp.where(j == 2, 3, j)) % n_t)
 
-    for i in range(copies):
-        remote(chunk(across, i), chunk(across, i), xf_send.at[i], xf_recv.at[i],
-               place(d, e, right)).wait_recv()
+    for i, h in steps:
+        arrives(band(across, i, h), xf_recv.at[i, h])
     features(across)
 
     gate, up, grad_act = pre[0], pre[1], pre[2]
@@ -260,7 +289,6 @@
         ys.append(first.astype(BF16))
         gs.append(second.astype(BF16))
     y, g = jnp.concatenate(ys, axis=1), jnp.concatenate(gs, axis=1)
-    sel0, sel1 = sel0_ref[...], sel1_ref[...]
     chosen0 = jnp.dot(sel0, y, preferred_element_type=F32)
     chosen1 = jnp.dot(sel1, y, preferred_element_type=F32)
     grad_mix = jnp.dot(sel0 + sel1, g, preferred_element_type=F32)
@@ -358,21 +386,9 @@
                place(d, e, right)).wait_recv()
         remote(gtok_all.at[other(o)], gtok_all.at[other(o)], gt_send.at[o - 1], gt_recv.at[o - 1],
                place(d, e, right)).wait_recv()
-    for q in range(n_t):
-        at = slice(q * width, (q + 1) * width)
-        mixed_ref[:, at] = mixed_all[q]
-        gtok_ref[:, at] = gtok_all[q]
     for o in range(1, n_t):
         remote(grads.at[other(o)], grads.at[other(o)], gx_send.at[o - 1], gx_recv.at[o - 1],
                place(d, e, right)).wait_recv()
-    for q in range(n_t):
-        for c in range(copies):
-            at = slice(q * width + c * LANES, q * width + (c + 1) * LANES)
-            for h in range(n_half):
-                a, b = unit(c * n_half + h)
-                grouter_ref[h * SLOTS : (h + 1) * SLOTS, at] = grads[q, a, b]
-            a, b = unit(n_half * copies + c // SLOTS)
-            ggain_ref[:, at] = grads[q, a, b, c % SLOTS : c % SLOTS + 1]
 
     a2a.wait_send()
     back_bulk.wait_send()
@@ -384,6 +400,26 @@
         copy.wait_send()
 
 
+def assemble_kernel(dims, mixed_all, gtok_all, grads, mixed_ref, gtok_ref, grouter_ref, ggain_ref):
+    n_dp, n_e, n_t, experts, copies = dims
+    width, n_half, units = copies * LANES, experts // SLOTS, grads.shape[2]
+
+    def unit(u):
+        return u // units, u % units
+
+    for q in range(n_t):
+        at = slice(q * width, (q + 1) * width)
+        mixed_ref[:, at] = mixed_all[q]
+        gtok_ref[:, at] = gtok_all[q]
+        for c in range(copies):
+            at = slice(q * width + c * LANES, q * width + (c + 1) * LANES)
+            for h in range(n_half):
+                a, b = unit(c * n_half + h)
+                grouter_ref[h * SLOTS : (h + 1) * SLOTS, at] = grads[q, a, b]
+            a, b = unit(n_half * copies + c // SLOTS)
+            ggain_ref[:, at] = grads[q, a, b, c % SLOTS : c % SLOTS + 1]
+
+
 def shards(dims, tokens, cotangent, gain, w_router, w_gate, w_up, w_down, expert_ids, slots):
     n_dp, n_e, n_t, experts, copies = dims
     count, features = tokens.shape
@@ -391,12 +427,6 @@
     width = features // n_t
     n_rows = n_e * SLOTS
     n_line, n_z = n_dp * LINE, n_e // LINE
-    row_index = expert_ids * SLOTS + slots
-    tile = jnp.arange(experts * SLOTS, dtype=jnp.int32)
-    sel = [(row_index[:, c : c + 1] == tile[None, :]).astype(BF16) for c in range(2)]
-    sel_t = [(row_index[:, c][None, :] == tile[:, None]).astype(BF16) for c in range(2)]
-    columns = jnp.arange(experts, dtype=jnp.int32)[None, :]
-    sign = (expert_ids[:, 0:1] == columns).astype(F32) - (expert_ids[:, 1:2] == columns).astype(F32)
     units = -(-(copies * (experts // SLOTS) + -(-copies // SLOTS)) // n_line)
     block = (n_e, 8, LANES)
     dma = pltpu.SemaphoreType.DMA
@@ -414,29 +444,36 @@
         pltpu.VMEM((copies,) + block, BF16),
         pltpu.VMEM(block, BF16),
         pltpu.VMEM((experts, copies, 8, LANES), BF16),
-        pltpu.VMEM((n_t, count, width), BF16), pltpu.VMEM((n_t, count, width), BF16),
         pltpu.VMEM((count, LANES), F32), pltpu.VMEM((n_t - 1, count, LANES), F32),
         pltpu.VMEM((n_line, units, SLOTS, LANES), F32), pltpu.VMEM((n_line, units, SLOTS, LANES), F32),
         pltpu.VMEM((units, SLOTS, LANES), F32),
         pltpu.VMEM((n_z, units, SLOTS, LANES), F32), pltpu.VMEM((units, SLOTS, LANES), F32),
-        pltpu.VMEM((n_t, n_line, units, SLOTS, LANES), F32),
         dma((3,)), dma((2,)),
-    ] + [dma((copies,))] * 16 + [dma((2,))] + [dma((n_t - 1,))] * 6 + [dma((2,))] * 3 + [dma((n_t - 1,))] * 2
+    ] + [dma((copies, BANDS))] * 8 + [dma((copies,))] * 8 + [dma((2,))] + [dma((n_t - 1,))] * 6 + [dma((2,))] * 3 + [dma((n_t - 1,))] * 2
+    gathered = pl.pallas_call(
+        functools.partial(layer_kernel, dims),
+        out_shape=(
+            jax.ShapeDtypeStruct((n_t, count, width), BF16), jax.ShapeDtypeStruct((n_t, count, width), BF16),
+            jax.ShapeDtypeStruct((n_t, n_line, units, SLOTS, LANES), F32),
+        ),
+        in_specs=[vmem] * 6 + [pl.BlockSpec(memory_space=pl.ANY)] * 3,
+        out_specs=(vmem,) * 3,
+        scratch_shapes=scratch,
+        compiler_params=pltpu.CompilerParams(
+            collective_id=0, has_side_effects=True, vmem_limit_bytes=56 * 1024 * 1024),
+    )(
+        tokens, cotangent, gain.reshape(1, features), w_router.T, expert_ids.T, slots.T,
+        w_gate.reshape(n_t, width, hidden), w_up.reshape(n_t, width, hidden), w_down.reshape(hidden, features),
+    )
     mixed, gtok, grouter, ggain = pl.pallas_call(
-        functools.partial(layer_kernel, dims),
+        functools.partial(assemble_kernel, dims),
         out_shape=(
             jax.ShapeDtypeStruct((count, features), BF16), jax.ShapeDtypeStruct((count, features), BF16),
             jax.ShapeDtypeStruct((experts, features), F32), jax.ShapeDtypeStruct((1, features), F32),
         ),
-        in_specs=[vmem] * 9 + [pl.BlockSpec(memory_space=pl.ANY)] * 3,
+        in_specs=[vmem] * 3,
         out_specs=(vmem,) * 4,
-        scratch_shapes=scratch,
-        compiler_params=pltpu.CompilerParams(
-            collective_id=0, has_side_effects=True, vmem_limit_bytes=56 * 1024 * 1024),
-    )(
-        tokens, cotangent, gain.reshape(1, features), w_router.T, sel[0], sel[1], sel_t[0], sel_t[1], sign,
-        w_gate.reshape(n_t, width, hidden), w_up.reshape(n_t, width, hidden), w_down.reshape(hidden, features),
-    )
+    )(*gathered)
     return mixed, gtok, grouter.T, ggain.reshape(features)
 
 

time: 143 us -> 129 us (0.902)
  local copies, waits for them, and re-layouts: 6.69 us -> 0 us
  Pallas kernels: 133 us -> 128 us
  other arithmetic: 2.64 us -> 0 us
    pallas_call x1, Pallas kernels: 133 us -> 126 us  [shards(): pl.pallas_call(functools.partial(layer_kernel, dims), out_shape=(jax.Shap...]
    unnamed x4 -> x0, local copies, waits for them, and re-layouts: 5.92 us -> none
    pallas_call x0 -> x1, Pallas kernels: none -> 1.72 us  [shards(): pl.pallas_call(functools.partial(assemble_kernel, dims), out_shape=(jax.S...]
where the time goes in v3:
time: 129 us
  Pallas kernels  128 us (99%)
    pallas_call x1, Pallas kernels, shards(): pl.pallas_call(functools.partial(layer_kernel, dims), out_shape=(jax.Shap...  126 us

profile of v3, /device:TPU:1, one launch (start us, length us, event | category | flops | bytes accessed | tf_op | source)
XLA Modules:
  0.0 128.5 jit_solution(8461924305983589392)
XLA Ops:
  0.6 126.2 %shard_map.120 = (bf16[4,16,768]{2,1,0:T(8,128)(2,1)}, bf16[4,16,768]{2,1,0:T(8,128)(2,1)}, f32[4,16,1,4,128]{4,3,2,1,0:T(4,128)}) custom-call(bf16[16,3072]{1,0:T(8,128)(2,1)} %tokens_ref.1, bf16[16,3072]{1,0:T(8,128)(2,1)} %cot_ref.1, f32[1,3072]{1,0:T(1,128)} %bitcast.13, bf16[8,3072]{1,0:T(8,128)(2,1)} %bitcast.12, s32[2,16]{1,0:T(2,128)} %bitcast.14, ...), custom_call_target="tpu_custom_call" | custom-call | tf_op jit(solution)/shard_map/pallas_call | solution.py:453
  126.8 1.7 %shard_map.121 = (bf16[16,3072]{1,0:T(8,128)(2,1)}, bf16[16,3072]{1,0:T(8,128)(2,1)}, f32[8,3072]{1,0:T(8,128)}, f32[1,3072]{1,0:T(1,128)}) custom-call(bf16[4,16,768]{2,1,0:T(8,128)(2,1)} %get-tuple-element.11.mixed_all, bf16[4,16,768]{2,1,0:T(8,128)(2,1)} %get-tuple-element.12.gtok_all, f32[4,16,1,4,128]{4,3,2,1,0:T(4,128)} %get-tuple-element.13.grads), custom_call_target="tpu_custom_call" | custom-call | tf_op jit(solution)/shard_map/pallas_call | solution.py:468

commit v4 on v3

--- a/solution.py
+++ b/solution.py
@@ -61,6 +61,29 @@
     return sel0, sel1, sign, picks[0].astype(BF16), picks[1].astype(BF16)
 
 
+def swapped(k, s, copies):
+    if copies != 6:
+        return s
+    a = 1 + 2 * modulo(k, 2)
+
+    def equal(n):
+        return divide(copies - modulo(s - n + copies, copies), copies)
+
+    return s + equal(a) - equal(a + 1)
+
+
+def far_first(n):
+    return sorted(range(1, n), key=lambda i: -min(i, n - i))
+
+
+def divide(a, n):
+    return lax.div(a, jnp.int32(n))
+
+
+def modulo(a, n):
+    return lax.rem(a, jnp.int32(n))
+
+
 def layer_kernel(
     dims,
     tokens_ref, cot_ref, gain_ref, router_ref, ids_ref, slots_ref,
@@ -76,11 +99,13 @@
     width = copies * LANES
     half = copies // 2
     d, e, t = lax.axis_index("dp"), lax.axis_index("expert"), lax.axis_index("tensor")
-    k, s = e // copies, e % copies
+    k = e // copies
+    p = swapped(k, e % copies, copies)
+    pair = p // 2 * 2
     z, line = e // LINE, d * LINE + e % LINE
     n_z, n_line = n_e // LINE, n_dp * LINE
     left, right, across = (t + n_t - 1) % n_t, (t + 1) % n_t, (t + 2) % n_t
-    mine = t * copies + s
+    mine = pl.ds(t * copies + pair, 2)
     sl = pl.ds(pl.multiple_of(t * width, LANES), width)
 
     def place(dp, expert, tensor):
@@ -99,12 +124,26 @@
     for w in weights:
         w.start()
 
+    rows_of = [modulo(modulo(e, LINE) + dy, LINE) for dy in range(LINE)]
+    plane_of = [modulo(z + dz, n_z) * LINE for dz in range(n_z)]
+
+    def to_everyone(send):
+        near = far_first(LINE)
+
+        @pl.loop(1, n_z)
+        def _(i):
+            dz = divide(i, 2) * (1 - 2 * modulo(i, 2)) + n_z // 2
+            base = modulo(z + dz + n_z, n_z) * LINE
+            for dy in near + [0]:
+                send(base + rows_of[dy])
+
+        for dy in near:
+            send(z * LINE + rows_of[dy])
+
     bar = pltpu.get_barrier_semaphore()
 
-    @pl.loop(1, n_e)
-    def _(i):
-        pl.semaphore_signal(bar, inc=1, device_id=place(d, (e + i) % n_e, t),
-                            device_id_type=pl.DeviceIdType.MESH)
+    to_everyone(lambda to: pl.semaphore_signal(
+        bar, inc=1, device_id=place(d, to, t), device_id_type=pl.DeviceIdType.MESH))
 
     for o in range(1, n_t):
         pl.semaphore_signal(bar, inc=1, device_id=place(d, e, (t + o) % n_t),
@@ -136,13 +175,16 @@
 
     pl.semaphore_wait(bar, n_e - 1 + n_t - 1 + (n_dp - 1) * LINE)
 
-    @pl.loop(1, n_e)
-    def _(i):
-        to = (e + i) % n_e
-        remote(packed.at[to // copies, to % copies], arrived.at[t * copies + to % copies, e],
+    def hand_out(to):
+        expert = divide(to, copies)
+        both = divide(swapped(expert, to - expert * copies, copies), 2) * 2
+        remote(packed.at[expert, pl.ds(both, 2)], arrived.at[pl.ds(t * copies + both, 2), e],
                a2a_sem.at[0], a2a_sem.at[1], place(d, to, t)).start()
 
-    arrived[mine, e] = packed[k, s]
+    to_everyone(hand_out)
+
+    for i in range(2):
+        arrived[t * copies + pair + i, e] = packed[k, pair + i]
     scaled = floats * gain_ref[...]
     router = router_ref[...].astype(F32)
     through = jnp.concatenate(
@@ -153,7 +195,10 @@
     a2a.wait_recv()
 
     def piece(i):
-        return (s + i) % copies
+        return (pair + i) % copies
+
+    def holder(q):
+        return k * copies + swapped(k, q, copies)
 
     started = []
 
@@ -171,9 +216,10 @@
         remote(block, block, cp_send.at[0, 0], recv, place(d, e, right)).wait_recv()
 
     def to_copies(h):
-        for i in range(1, copies):
-            own = band(t, 0, h)
-            go(remote(own, own, cp_send.at[i, h], cp_recv.at[s, h], place(d, k * copies + piece(copies - i), t)))
+        for i in range(2, copies):
+            to = (pair + (copies - 2 if i < 4 else 2) + i % 2) % copies
+            own = arrived.at[t * copies + p, pl.ds(h * span, span)]
+            go(remote(own, own, cp_send.at[i, h], cp_recv.at[p, h], place(d, holder(to), t)))
 
     to_copies(0)
 
@@ -188,10 +234,11 @@
         block, to = (band(left, i, h), right) if i < half else (band(right, i, h), left)
         go(remote(block, block, xf_send.at[i, h], xf_recv.at[i, h], place(d, e, to)))
 
-    steps = [(i, h) for h in range(bands) for i in range(copies)]
+    steps = ([(i, h) for h in range(bands) for i in range(2)]
+             + [(i, h) for h in range(bands) for i in range(2, copies)])
     waiting = []
     for i, h in steps:
-        if i > 0:
+        if i > 1:
             arrives(band(t, i, h), cp_recv.at[piece(i), h])
         both_ways(i, h)
         if i == AHEAD and h + 1 < bands:
@@ -243,6 +290,10 @@
             parts[q, c] = join_rows(y[:, at], g[:, at]).astype(BF16)
 
     order = [(i + 1) % copies for i in range(copies)]
+
+    def piece(i):
+        return (p + i) % copies
+
     quarter(across)
     for i in order:
         src = parts.at[across, piece(i)]
@@ -266,19 +317,17 @@
         reduced[i] = total.astype(BF16)
         if i > 0:
             go(remote(reduced.at[i], copy_in.at[i], c_send.at[i], c_recv.at[i],
-                      place(d, k * copies + piece(i), t)))
+                      place(d, holder(piece(i)), t)))
     total = reduced[0].astype(F32)
     for i in range(1, copies):
         remote(copy_in.at[i], copy_in.at[i], c_send.at[i], c_recv.at[i], place(d, e, right)).wait_recv()
         total = total + copy_in[i].astype(F32)
     finished[...] = total.astype(BF16)
 
-    @pl.loop(1, n_e)
-    def _(i):
-        to = (e + i) % n_e
-        remote(finished.at[to], back.at[k, s], back_sem.at[0], back_sem.at[1], place(d, to, t)).start()
-
-    back[k, s] = finished[e]
+    to_everyone(lambda to: remote(
+        finished.at[to], back.at[k, p], back_sem.at[0], back_sem.at[1], place(d, to, t)).start())
+
+    back[k, p] = finished[e]
     bulk = arrived.at[0, pl.ds(0, n_e - 1)]
     back_bulk = remote(bulk, bulk, back_sem.at[0], back_sem.at[1], place(d, e, right))
     back_bulk.wait_recv()
@@ -332,13 +381,15 @@
         a, b = unit(n_half * copies + c // SLOTS)
         sums[a, b, c % SLOTS : c % SLOTS + 1] = gain_part[:, at]
 
-    def member(i):
-        j = (line + i) % n_line
-        return j, place(j // LINE, z * LINE + j % LINE, t)
-
-    @pl.loop(1, n_line)
-    def _(i):
-        j, target = member(i)
+    near = far_first(LINE) + [0]
+    members = []
+    for dy in near:
+        for dd in range(n_dp):
+            if dy or dd:
+                there = modulo(d + dd, n_dp)
+                members.append((there * LINE + rows_of[dy], place(there, z * LINE + rows_of[dy], t)))
+
+    for j, target in members:
         remote(sums.at[j], line_in.at[line], line_sem.at[0], line_sem.at[1], target).start()
 
     mean = (scalars[:, 1:2] + jnp.sum(grad_logits * through, axis=1, keepdims=True)) / (n_t * width)
@@ -354,10 +405,8 @@
     line_sum[...] = jnp.sum(line_in[...], axis=0)
 
     if n_z > 1:
-        @pl.loop(1, n_z)
-        def _(i):
-            to = (z + i) % n_z
-            remote(line_sum, z_in.at[z], z_sem.at[0], z_sem.at[1], place(d, to * LINE + e % LINE, t)).start()
+        for dz in far_first(n_z):
+            remote(line_sum, z_in.at[z], z_sem.at[0], z_sem.at[1], place(d, plane_of[dz] + rows_of[0], t)).start()
 
         z_in[z] = line_sum[...]
         zs = pl.ds(0, n_z - 1)
@@ -367,9 +416,7 @@
     else:
         z_sum[...] = line_sum[...]
 
-    @pl.loop(1, n_line)
-    def _(i):
-        j, target = member(i)
+    for j, target in members:
         remote(z_sum, grads.at[t, line], gl_sem.at[0], gl_sem.at[1], target).start()
 
     grads[t, line] = z_sum[...]

time: 129 us -> 124 us (0.961)
  Pallas kernels: 128 us -> 123 us
    pallas_call x1, Pallas kernels: 126 us -> 122 us  [shards(): pl.pallas_call(functools.partial(layer_kernel, dims), out_shape=(jax.Shap...]
where the time goes in v4:
time: 124 us
  Pallas kernels  123 us (99%)
    pallas_call x1, Pallas kernels, shards(): pl.pallas_call(functools.partial(layer_kernel, dims), out_shape=(jax.Shap...  122 us

profile of v4, /device:TPU:1, one launch (start us, length us, event | category | flops | bytes accessed | tf_op | source)
XLA Modules:
  0.0 123.9 jit_solution(12519256275403107645)
XLA Ops:
  0.6 121.5 %shard_map.120 = (bf16[4,16,768]{2,1,0:T(8,128)(2,1)}, bf16[4,16,768]{2,1,0:T(8,128)(2,1)}, f32[4,16,1,4,128]{4,3,2,1,0:T(4,128)}) custom-call(bf16[16,3072]{1,0:T(8,128)(2,1)} %tokens_ref.1, bf16[16,3072]{1,0:T(8,128)(2,1)} %cot_ref.1, f32[1,3072]{1,0:T(1,128)} %bitcast.13, bf16[8,3072]{1,0:T(8,128)(2,1)} %bitcast.12, s32[2,16]{1,0:T(2,128)} %bitcast.14, ...), custom_call_target="tpu_custom_call" | custom-call | tf_op jit(solution)/shard_map/pallas_call | solution.py:500
  122.2 1.7 %shard_map.121 = (bf16[16,3072]{1,0:T(8,128)(2,1)}, bf16[16,3072]{1,0:T(8,128)(2,1)}, f32[8,3072]{1,0:T(8,128)}, f32[1,3072]{1,0:T(1,128)}) custom-call(bf16[4,16,768]{2,1,0:T(8,128)(2,1)} %get-tuple-element.11.mixed_all, bf16[4,16,768]{2,1,0:T(8,128)(2,1)} %get-tuple-element.12.gtok_all, f32[4,16,1,4,128]{4,3,2,1,0:T(4,128)} %get-tuple-element.13.grads), custom_call_target="tpu_custom_call" | custom-call | tf_op jit(solution)/shard_map/pallas_call | solution.py:515

commit v5 on v4

--- a/solution.py
+++ b/solution.py
@@ -12,7 +12,7 @@
 SLOTS = 4
 LINE = 4
 BANDS = 3
-LAG = 3
+LAG = 7
 AHEAD = 2
 F32 = jnp.float32
 BF16 = jnp.bfloat16
@@ -246,9 +246,6 @@
         waiting.append((i, h))
         if len(waiting) > LAG:
             pass_on(*waiting.pop(0))
-    for i, h in waiting:
-        pass_on(i, h)
-
     pre[...] = jnp.zeros_like(pre)
     for w in weights:
         w.wait()
@@ -265,9 +262,13 @@
         down = wd[:, pl.ds(pl.multiple_of(q * width, LANES), width)]
         pre[2] += lax.dot_general(g, down, NT, preferred_element_type=F32)
 
-    @pl.loop(0, n_t - 1)
+    features(t)
+    for i, h in waiting:
+        pass_on(i, h)
+
+    @pl.loop(0, 2)
     def _(j):
-        features((t + jnp.where(j == 2, 3, j)) % n_t)
+        features((t + 1 + 2 * j) % n_t)
 
     for i, h in steps:
         arrives(band(across, i, h), xf_recv.at[i, h])
@@ -289,7 +290,7 @@
             at = slice(c * LANES, (c + 1) * LANES)
             parts[q, c] = join_rows(y[:, at], g[:, at]).astype(BF16)
 
-    order = [(i + 1) % copies for i in range(copies)]
+    order = [i for pair_of in zip(range(1, half), range(half, copies)) for i in pair_of] + [copies - 1, 0]
 
     def piece(i):
         return (p + i) % copies
@@ -299,16 +300,25 @@
         src = parts.at[across, piece(i)]
         go(remote(src, fwd_in.at[i], f_send.at[i], f_recv.at[i], place(d, e, right if i < half else left)))
 
-    @pl.loop(0, 3)
+    @pl.loop(0, 2)
     def _(j):
-        quarter((t + jnp.where(j == 0, 1, jnp.where(j == 1, n_t - 1, 0))) % n_t)
+        quarter((t + 1 + 2 * j) % n_t)
+
+    def to_right(i):
+        go(remote(parts.at[right, piece(i)], left_in.at[i], r_send.at[i], r_recv.at[i], place(d, e, right)))
+
+    def to_left(i):
+        go(remote(parts.at[left, piece(i)], right_in.at[i], l_send.at[i], l_recv.at[i], place(d, e, left)))
+
+    for i in order:
+        to_left(i) if i < half else to_right(i)
+    quarter(t)
 
     for i in order:
         remote(fwd_in.at[i], fwd_in.at[i], f_send.at[i], f_recv.at[i], place(d, e, right)).wait_recv()
         on = right if i < half else left
         parts[on, piece(i)] = (parts[on, piece(i)].astype(F32) + fwd_in[i].astype(F32)).astype(BF16)
-        go(remote(parts.at[right, piece(i)], left_in.at[i], r_send.at[i], r_recv.at[i], place(d, e, right)))
-        go(remote(parts.at[left, piece(i)], right_in.at[i], l_send.at[i], l_recv.at[i], place(d, e, left)))
+        to_right(i) if i < half else to_left(i)
 
     for i in order:
         remote(left_in.at[i], left_in.at[i], r_send.at[i], r_recv.at[i], place(d, e, right)).wait_recv()

time: 124 us -> 129 us (1.040)
  Pallas kernels: 123 us -> 128 us
    pallas_call x1, Pallas kernels: 122 us -> 126 us  [shards(): pl.pallas_call(functools.partial(layer_kernel, dims), out_shape=(jax.Shap...]
where the time goes in v5:
time: 129 us
  Pallas kernels  128 us (99%)
    pallas_call x1, Pallas kernels, shards(): pl.pallas_call(functools.partial(layer_kernel, dims), out_shape=(jax.Shap...  126 us

profile of v5, /device:TPU:1, one launch (start us, length us, event | category | flops | bytes accessed | tf_op | source)
XLA Modules:
  0.0 128.6 jit_solution(13002123721133729106)
XLA Ops:
  0.6 126.2 %shard_map.120 = (bf16[4,16,768]{2,1,0:T(8,128)(2,1)}, bf16[4,16,768]{2,1,0:T(8,128)(2,1)}, f32[4,16,1,4,128]{4,3,2,1,0:T(4,128)}) custom-call(bf16[16,3072]{1,0:T(8,128)(2,1)} %tokens_ref.1, bf16[16,3072]{1,0:T(8,128)(2,1)} %cot_ref.1, f32[1,3072]{1,0:T(1,128)} %bitcast.13, bf16[8,3072]{1,0:T(8,128)(2,1)} %bitcast.12, s32[2,16]{1,0:T(2,128)} %bitcast.14, ...), custom_call_target="tpu_custom_call" | custom-call | tf_op jit(solution)/shard_map/pallas_call | solution.py:510
  126.9 1.7 %shard_map.121 = (bf16[16,3072]{1,0:T(8,128)(2,1)}, bf16[16,3072]{1,0:T(8,128)(2,1)}, f32[8,3072]{1,0:T(8,128)}, f32[1,3072]{1,0:T(1,128)}) custom-call(bf16[4,16,768]{2,1,0:T(8,128)(2,1)} %get-tuple-element.11.mixed_all, bf16[4,16,768]{2,1,0:T(8,128)(2,1)} %get-tuple-element.12.gtok_all, f32[4,16,1,4,128]{4,3,2,1,0:T(4,128)} %get-tuple-element.13.grads), custom_call_target="tpu_custom_call" | custom-call | tf_op jit(solution)/shard_map/pallas_call | solution.py:525
